TPU v7x, 32 devices: a whole 2x2x4 slice. The times are simulated.
32 devices in a mesh: group: 1, ctx: 32 (over z, y, x, core).
Axes of the slice: x: 2, y: 2, z: 4, core: 2. Of those that a mesh axis runs over, the one named last changes fastest.
Arguments:
- queries: bfloat16 [2, 64, 128], P('group'), may hold values from -80 to 80
- key_cache: bfloat16 [2, 4096, 512], P('group', 'ctx'), may hold values from -4 to 4
- value_cache: bfloat16 [2, 4096, 512], P('group', 'ctx'), may hold values from -6 to 6
- out_weight: bfloat16 [8192, 4096], P('ctx'), may hold values from -0.125 to 0.125
- hidden_in: bfloat16 [2, 4096], P('group'), may hold values from -45 to 45
- norm_gain: float32 [4096], replicated, may hold values from 0.25 to 1.75
- gate_weight: bfloat16 [32, 4096, 192], P('ctx'), may hold values from -0.09375 to 0.09375
- up_weight: bfloat16 [32, 4096, 192], P('ctx'), may hold values from -0.09375 to 0.09375
- down_weight: bfloat16 [32, 192, 4096], P('ctx'), may hold values from -0.15625 to 0.15625
- routes: int32 [2, 4], P('group'), may hold values from 0 to 3, all different within a row; in each aligned block of 2 rows (0 to 1, 2 to 3, ...) at most 2 rows name the same one
- route_weight: float32 [2, 4], P('group'), may hold values from 0.1 to 1
Outputs:
- mixed: float32 [2, 4096], P('group', 'ctx')
Inputs may be any that keep to these rules, and one draw needn't show every extreme that they name: `routes`: each row names 4 different experts; no expert is named by more than 2 rows, a bound that some block reaches.
All inputs are finite; a program needn't handle non-finite values.
Results may differ from a plain program's by a relative error of at most 0.0035.
Values may be sent and summed in bfloat16 or wider, within the bound.
No kernel may reach another device: no remote copies, remote signals or barrier semaphores. Data moves between devices by JAX's collectives and lax.ppermute only.
A program may use at most 64 MiB of HBM per device.

v0:
```python
import jax
import jax.numpy as jnp
from jax import lax
from jax.sharding import PartitionSpec as P

QUARTERS = 8


eps = 1e-06


def slot_numbers(routes, expert_count):
    flat_routes = routes.reshape(-1)
    onehot = (flat_routes[:, None] == jnp.arange(expert_count, dtype=jnp.int32)[None, :]).astype(
        jnp.int32
    )
    before = jnp.cumsum(onehot, axis=0) - onehot
    return jnp.sum(before * onehot, axis=1)


def body(
    queries,
    key_cache,
    value_cache,
    out_weight,
    hidden_in,
    norm_gain,
    gate_weight,
    up_weight,
    down_weight,
    routes,
    route_weight,
):
    devices = lax.axis_size("ctx")
    my_index = lax.axis_index("ctx")
    seq_count, head_count, head_dim = queries.shape
    kv_heads = key_cache.shape[2] // head_dim
    group_size = head_count // kv_heads
    model_width = hidden_in.shape[1]
    local_len = key_cache.shape[1]
    query_view = queries.reshape(seq_count, kv_heads, group_size, head_dim)
    key_view = key_cache.reshape(seq_count, local_len, kv_heads, head_dim)
    value_view = value_cache.reshape(seq_count, local_len, kv_heads, head_dim)
    scores = jnp.einsum(
        "sgjd,scgd->sgjc", query_view, key_view, preferred_element_type=jnp.float32
    ) * head_dim ** (-0.5)
    row_peak = lax.pmax(jnp.max(scores, axis=-1), "ctx")
    numer = jnp.exp(scores - row_peak[..., None])
    denom_part = jnp.sum(numer, axis=-1)
    partial_value = jnp.einsum(
        "sgjc,scgd->sgjd",
        numer.astype(jnp.bfloat16),
        value_view,
        preferred_element_type=jnp.float32,
    )
    partial_value = partial_value.reshape(seq_count, head_count * head_dim)
    feat_dev = head_count * head_dim // devices
    feat_start = my_index * feat_dev
    summed, denoms = lax.psum((partial_value, denom_part), "ctx")
    attn_mine = lax.dynamic_slice_in_dim(summed, feat_start, feat_dev, 1)
    spread_denoms = jnp.repeat(denoms.reshape(seq_count, head_count), head_dim, axis=1)
    mine_denoms = lax.dynamic_slice_in_dim(spread_denoms, feat_start, feat_dev, 1)
    attended = (attn_mine / mine_denoms).astype(jnp.bfloat16)
    proj_part = jnp.dot(attended, out_weight, preferred_element_type=jnp.float32)
    col_dev = model_width // devices
    col_start = my_index * col_dev
    projected = lax.psum(proj_part, "ctx")
    resid = hidden_in.astype(jnp.float32) + projected
    inverse_rms = lax.rsqrt(jnp.mean(resid * resid, axis=-1, keepdims=True) + eps)
    normed = (resid * inverse_rms * norm_gain).astype(jnp.bfloat16)
    resid_mine = lax.dynamic_slice_in_dim(resid, col_start, col_dev, 1)
    expert_count = devices // QUARTERS
    top_count = routes.shape[1]
    capacity = min(2 * seq_count * top_count // expert_count, seq_count)
    expert = my_index // QUARTERS
    slot_index = slot_numbers(routes, expert_count)
    flat_routes = routes.reshape(-1)
    token_of = jnp.arange(seq_count * top_count, dtype=jnp.int32) // top_count
    matches = (
        (flat_routes[None, :] == expert)
        & (slot_index[None, :] == jnp.arange(capacity, dtype=jnp.int32)[:, None])
    ).astype(jnp.float32)
    owners = (token_of[:, None] == jnp.arange(seq_count, dtype=jnp.int32)[None, :]).astype(
        jnp.float32
    )
    select = jnp.dot(matches, owners, precision=lax.Precision.HIGHEST)
    slot_weight = jnp.dot(matches, route_weight.reshape(-1), precision=lax.Precision.HIGHEST)
    picked_rows = jnp.dot(
        select.astype(jnp.bfloat16), normed, preferred_element_type=jnp.float32
    ).astype(jnp.bfloat16)
    gate_act = jnp.dot(picked_rows, gate_weight[0], preferred_element_type=jnp.float32)
    up_act = jnp.dot(picked_rows, up_weight[0], preferred_element_type=jnp.float32)
    hidden = (jax.nn.silu(gate_act) * up_act).astype(jnp.bfloat16)
    expert_out = (
        jnp.dot(hidden, down_weight[0], preferred_element_type=jnp.float32) * slot_weight[:, None]
    )
    received = lax.all_to_all(
        expert_out.astype(jnp.bfloat16), "ctx", split_axis=1, concat_axis=0, tiled=True
    ).astype(expert_out.dtype)
    quarter_ids = jnp.arange(QUARTERS, dtype=jnp.int32)[None, None, :]
    shard_rows = (routes[:, :, None] * QUARTERS + quarter_ids) * capacity + slot_index.reshape(
        seq_count, top_count
    )[:, :, None]
    moe_mine = jnp.sum(received[shard_rows], axis=(1, 2))
    return resid_mine + moe_mine


def solution(mesh):
    in_specs = (
        P("group", None, None),
        P("group", "ctx", None),
        P("group", "ctx", None),
        P("ctx", None),
        P("group", None),
        P(),
        P("ctx", None, None),
        P("ctx", None, None),
        P("ctx", None, None),
        P("group", None),
        P("group", None),
    )
    out_specs = P("group", "ctx")
    return jax.shard_map(body, mesh=mesh, in_specs=in_specs, out_specs=out_specs, check_vma=False)
```

profile of v0, /device:TPU:0, one launch (start us, length us, event | category | flops | bytes accessed | tf_op | source)
XLA Modules:
  0.0 239.1 jit_solution(7500703949883063939)
XLA Ops:
  6.5 1.4 fusion.41
  8.0 42.0 %pmax.7 = f32[2,4,16]{2,1,0:T(4,128)S(1)} all-reduce(f32[2,4,16]{2,1,0:T(4,128)S(1)} %get-tuple-element.7), channel_id=1, replica_groups=mesh['group'=1,'ctx'=32] {'ctx'}, use_global_device_ids=true, to_apply=%region_1.0 | all-reduce | flops 128 | bytes 1024 | tf_op jit(solution)/shard_map/pmax | solution.py:47
  50.0 1.2 fusion.17
  51.2 0.7 copy.38
  51.9 0.8 broadcast_in_dim_reshape.2
  52.7 0.7 broadcast_multiply_fusion
  53.3 0.2 fusion.22
  53.6 0.8 reshape.100
  54.3 0.2 reduce_window_sum.11
  54.7 40.0 %psum.22 = f32[2,64]{1,0:T(2,128)S(1)} all-reduce(f32[2,64]{1,0:T(2,128)S(1)} %reshape.87), channel_id=1, replica_groups=mesh['group'=1,'ctx'=32] {'ctx'}, use_global_device_ids=true, to_apply=%region_4.0 | all-reduce | flops 128 | bytes 1024 | tf_op jit(solution)/shard_map/psum | solution.py:59
  94.8 0.2 convolution_convert_fusion.1
  95.1 0.1 convolution_bitcast_fusion
  95.2 0.1 reshape.93
  95.3 76.0 %all-reduce.2.cloned.1.call-done = f32[2,8192]{1,0:T(2,128)} async-done(((f32[2,8192]{1,0:T(2,128)}), f32[2,8192]{1,0:T(2,128)}) %all-reduce.2.cloned.1.call-update) | async-done | bytes 65552 | tf_op jit(solution)/shard_map/psum | solution.py:59
  171.4 1.1 fusion.32
  172.4 41.0 %psum.23 = f32[2,4096]{1,0:T(2,128)S(1)} all-reduce(f32[2,4096]{1,0:T(2,128)S(1)} %fusion.32), channel_id=1, replica_groups=mesh['group'=1,'ctx'=32] {'ctx'}, use_global_device_ids=true, to_apply=%region_5.0 | all-reduce | flops 8192 | bytes 65536 | tf_op jit(solution)/shard_map/psum | solution.py:67
  213.5 0.1 multiply_reduce_fusion
  213.6 0.2 convolution_convert_fusion
  213.8 1.9 fusion.4
  215.8 3.7 %fusion.6 = bf16[2,32,128]{2,0,1:T(2,128)(2,1)} fusion(bf16[1,192,4096]{2,1,0:T(8,128)(2,1)} %param.19, bf16[2,4096]{1,0:T(2,128)(2,1)S(1)} %convolution_convert_fusion, bf16[1,4096,192]{1,2,0:T(8,128)(2,1)} %param.18, f32[2]{0:T(128)S(1)} %convolution_bitcast_fusion, f32[2,192]{1,0:T(2,128)S(1)} %fusion.4), kind=kOutput, calls=%fused_computation.10 | convolution fusion | flops 6310144 | bytes 3180040 | tf_op jit(solution)/shard_map/dot_general | solution.py:95
  219.5 4.4 %all-to-all-start = ((bf16[2,32,128]{2,0,1:T(2,128)(2,1)}), bf16[2,32,128]{2,0,1:T(2,128)(2,1)S(1)}, u32[]{:S(2)}, u32[]{:S(2)}) async-start(bf16[2,32,128]{2,0,1:T(2,128)(2,1)} %fusion.6), calls=%async_computation | async-start | bytes 32768 | tf_op jit(solution)/shard_map/all_to_all | solution.py:97
  223.9 7.2 %all-to-all-done = bf16[2,32,128]{2,0,1:T(2,128)(2,1)S(1)} async-done(((bf16[2,32,128]{2,0,1:T(2,128)(2,1)}), bf16[2,32,128]{2,0,1:T(2,128)(2,1)S(1)}, u32[]{:S(2)}, u32[]{:S(2)}) %all-to-all-start) | async-done | bytes 16416 | tf_op jit(solution)/shard_map/all_to_all | solution.py:97
  231.1 0.6 gather_fusion
  231.7 0.6 dynamic-slice_add_fusion
  (21 shorter events, 0.5 us)
Async XLA Ops:
  6.5 164.8 %copy-start = (bf16[256,4096]{1,0:T(8,128)(2,1)S(1)}, bf16[256,4096]{1,0:T(8,128)(2,1)}, u32[]{:S(2)}) copy-start(bf16[256,4096]{1,0:T(8,128)(2,1)} %param.14) | copy-start | bytes 6291460
  6.5 164.8 %all-reduce.2.cloned.1.call-start = ((), (), s32[]{:S(2)}) async-start(), calls=%async_computation.1 | async-start | bytes 131072 | tf_op jit(solution)/shard_map/psum | solution.py:59
  50.0 163.5 %copy-start.1 = (bf16[2,4096]{1,0:T(2,128)(2,1)S(1)}, bf16[2,4096]{1,0:T(2,128)(2,1)}, u32[]{:S(2)}) copy-start(bf16[2,4096]{1,0:T(2,128)(2,1)} %param.15) | copy-start | bytes 49156
  50.0 163.6 %copy-start.2 = (f32[4096]{0:T(1024)S(1)}, f32[4096]{0:T(1024)}, u32[]{:S(2)}) copy-start(f32[4096]{0:T(1024)} %param.16) | copy-start | bytes 49156
  219.5 11.6 %all-to-all-start = ((bf16[2,32,128]{2,0,1:T(2,128)(2,1)}), bf16[2,32,128]{2,0,1:T(2,128)(2,1)S(1)}, u32[]{:S(2)}, u32[]{:S(2)}) async-start(bf16[2,32,128]{2,0,1:T(2,128)(2,1)} %fusion.6), calls=%async_computation | async-start | bytes 32768 | tf_op jit(solution)/shard_map/all_to_all | solution.py:97
Sparse Core Ops, SparseCore 0:
  52.0 119.3 all-reduce.1
where the time goes:
time: 240 us; the launch traced here: 239 us
  blocking collectives  123 us (51%)
  waiting for transfers between devices  83.2 us (35%)
  between operations  13.5 us (6%)
  matrix products  9.84 us (4%)
  starting transfers between devices  4.4 us (2%)
  local copies, waits for them, and re-layouts  3.2 us (1%)
    psum x1, waiting for transfers between devices, body(): summed, denoms = lax.psum((partial_value, denom_part), 'ctx')  76 us
    pmax x1, blocking collectives, body(): row_peak = lax.pmax(jnp.max(scores, axis=-1), 'ctx')  42 us
    psum x1, blocking collectives, body(): projected = lax.psum(proj_part, 'ctx')  41 us
    psum x1, blocking collectives, body(): summed, denoms = lax.psum((partial_value, denom_part), 'ctx')  40 us
    all_to_all x1, waiting for transfers between devices, body(): lax.all_to_all(expert_out.astype(jnp.bfloat16), 'ctx', split_axis=1, conc...  7.16 us
  transfers between devices with their start and end apart: 2, of which 2 were waited for; matrix products, arithmetic and copies ran while one was open for 1% of the time, Pallas kernels for 0%

commit v1 on v0

v1 whole, which is shorter than its diff:
```python
import jax
import jax.numpy as jnp
from jax import lax
from jax.sharding import PartitionSpec as P

QUARTERS = 8


eps = 1e-06


def swap_blocks(blocks):
    return lax.all_to_all(blocks, "ctx", split_axis=0, concat_axis=0, tiled=True)


def body(
    queries,
    key_cache,
    value_cache,
    out_weight,
    hidden_in,
    norm_gain,
    gate_weight,
    up_weight,
    down_weight,
    routes,
    route_weight,
):
    devices = lax.axis_size("ctx")
    my_index = lax.axis_index("ctx")
    seq_count, head_count, head_dim = queries.shape
    kv_heads = key_cache.shape[2] // head_dim
    group_size = head_count // kv_heads
    model_width = hidden_in.shape[1]
    local_len = key_cache.shape[1]
    query_view = queries.reshape(seq_count, kv_heads, group_size, head_dim)
    key_view = key_cache.reshape(seq_count, local_len, kv_heads, head_dim)
    value_view = value_cache.reshape(seq_count, local_len, kv_heads, head_dim)
    scores = jnp.einsum(
        "sgjd,scgd->sgjc", query_view, key_view, preferred_element_type=jnp.float32
    ) * head_dim ** (-0.5)
    peak = jnp.max(scores, axis=-1)
    numer = jnp.exp(scores - peak[..., None])
    denom = jnp.sum(numer, axis=-1)
    weighted = jnp.einsum(
        "sgjc,scgd->sgjd",
        numer.astype(jnp.bfloat16),
        value_view,
        preferred_element_type=jnp.float32,
    )
    feat_dev = head_count * head_dim // devices
    spread = max(1, head_dim // feat_dev)
    heads_dev = max(1, feat_dev // head_dim)
    width = feat_dev // heads_dev

    def by_owner(stat):
        stat = jnp.repeat(stat.reshape(seq_count, head_count), spread, axis=1)
        return stat.reshape(seq_count, devices, heads_dev).transpose(1, 0, 2)

    weighted = weighted.reshape(seq_count, devices, heads_dev, width).transpose(1, 0, 2, 3)
    stats = jnp.stack([by_owner(peak), by_owner(denom)], axis=-1)
    sent = jnp.concatenate(
        [weighted.reshape(devices, -1), stats.reshape(devices, -1)], axis=1
    )
    got = swap_blocks(sent)
    parts = got[:, : seq_count * feat_dev].reshape(devices, seq_count, heads_dev, width)
    stats = got[:, seq_count * feat_dev :].reshape(devices, seq_count, heads_dev, 2)
    peaks = stats[..., 0]
    scale = jnp.exp(peaks - jnp.max(peaks, axis=0))
    denoms = jnp.sum(scale * stats[..., 1], axis=0)
    summed = jnp.sum(scale[..., None] * parts, axis=0)
    attended = (summed / denoms[..., None]).reshape(seq_count, feat_dev).astype(jnp.bfloat16)
    proj_part = jnp.dot(attended, out_weight, preferred_element_type=jnp.float32)
    col_dev = model_width // devices
    col_start = my_index * col_dev

    def to_owner(rows):
        blocks = rows.reshape(seq_count, devices, col_dev).transpose(1, 0, 2)
        return jnp.sum(swap_blocks(blocks).astype(jnp.float32), axis=0)

    hidden_mine = lax.dynamic_slice_in_dim(hidden_in, col_start, col_dev, 1)
    resid_mine = hidden_mine.astype(jnp.float32) + to_owner(proj_part)
    resid = swap_blocks(jnp.broadcast_to(resid_mine, (devices, seq_count, col_dev)))
    resid = resid.transpose(1, 0, 2).reshape(seq_count, model_width)
    inverse_rms = lax.rsqrt(jnp.mean(resid * resid, axis=-1, keepdims=True) + eps)
    normed = (resid * inverse_rms * norm_gain).astype(jnp.bfloat16)
    expert = my_index // QUARTERS
    token_weight = jnp.sum(jnp.where(routes == expert, route_weight, 0.0), axis=1)
    gate_act = jnp.dot(normed, gate_weight[0], preferred_element_type=jnp.float32)
    up_act = jnp.dot(normed, up_weight[0], preferred_element_type=jnp.float32)
    hidden = (jax.nn.silu(gate_act) * up_act).astype(jnp.bfloat16)
    expert_out = (
        jnp.dot(hidden, down_weight[0], preferred_element_type=jnp.float32)
        * token_weight[:, None]
    )
    return resid_mine + to_owner(expert_out.astype(jnp.bfloat16))


def solution(mesh):
    in_specs = (
        P("group", None, None),
        P("group", "ctx", None),
        P("group", "ctx", None),
        P("ctx", None),
        P("group", None),
        P(),
        P("ctx", None, None),
        P("ctx", None, None),
        P("ctx", None, None),
        P("group", None),
        P("group", None),
    )
    out_specs = P("group", "ctx")
    return jax.shard_map(body, mesh=mesh, in_specs=in_specs, out_specs=out_specs, check_vma=False)
```

time: 240 us -> 56.8 us (0.24)
  blocking collectives: 123 us -> 8.87 us
  waiting for transfers between devices: 83.2 us -> 17.8 us
  between operations: 13.5 us -> 0.13 us
  starting transfers between devices: 4.4 us -> 12.5 us
  local copies, waits for them, and re-layouts: 3.2 us -> 6.21 us
    psum x2 -> x0, blocking collectives: 81 us -> none  [the longest x1 41 us: body(): projected = lax.psum(proj_part, 'ctx')]
    psum x1 -> x0, waiting for transfers between devices: 76 us -> none  [body(): summed, denoms = lax.psum((partial_value, denom_part), 'ctx')]
    pmax x1 -> x0, blocking collectives: 42 us -> none  [body(): row_peak = lax.pmax(jnp.max(scores, axis=-1), 'ctx')]
    all_to_all x1 -> x3, waiting for transfers between devices: 7.16 us -> 17.8 us  [swap_blocks(): lax.all_to_all(blocks, 'ctx', split_axis=0, concat_axis=0, tiled=True)]
    all_to_all x0 -> x1, blocking collectives: none -> 8.87 us  [swap_blocks(): lax.all_to_all(blocks, 'ctx', split_axis=0, concat_axis=0, tiled=True)]
    all_to_all x1 -> x3, starting transfers between devices: 4.39 us -> 12.5 us  [swap_blocks(): lax.all_to_all(blocks, 'ctx', split_axis=0, concat_axis=0, tiled=True)]
    dot_general x0 -> x1, local copies, waits for them, and re-layouts: none -> 4.11 us  [body(): jnp.dot(attended, out_weight, preferred_element_type=jnp.float32)]
  transfers between devices with their start and end apart: 2 -> 3, of which waited for: 2 -> 3; matrix products, arithmetic and copies ran while one was open for 1% -> 7% of each run, Pallas kernels for 0% -> 0%
where the time goes in v1:
time: 56.8 us; the launch traced here: 56.4 us
  waiting for transfers between devices  17.8 us (31%)
  starting transfers between devices  12.5 us (22%)
  blocking collectives  8.87 us (16%)
  matrix products  8.62 us (15%)
  local copies, waits for them, and re-layouts  6.21 us (11%)
  other arithmetic  2.26 us (4%)
    all_to_all x3, waiting for transfers between devices, swap_blocks(): lax.all_to_all(blocks, 'ctx', split_axis=0, concat_axis=0, tiled=True)  17.8 us
    all_to_all x3, starting transfers between devices, swap_blocks(): lax.all_to_all(blocks, 'ctx', split_axis=0, concat_axis=0, tiled=True)  12.5 us
    all_to_all x1, blocking collectives, swap_blocks(): lax.all_to_all(blocks, 'ctx', split_axis=0, concat_axis=0, tiled=True)  8.87 us
    dot_general x1, local copies, waits for them, and re-layouts, body(): jnp.dot(attended, out_weight, preferred_element_type=jnp.float32)  4.11 us
    dot_general x1, matrix products, body(): jnp.dot(attended, out_weight, preferred_element_type=jnp.float32)  2.85 us
    dot_general x1, matrix products, body(): jnp.dot(hidden, down_weight[0], preferred_element_type=jnp.float32)  2.66 us
    dot_general x1, matrix products, body(): jnp.einsum('sgjd,scgd->sgjc', query_view, key_view, preferred_element_typ...  1.39 us
    dot_general x1, matrix products, body(): jnp.einsum('sgjc,scgd->sgjd', numer.astype(jnp.bfloat16), value_view, pre...  1.2 us
  transfers between devices with their start and end apart: 3, of which 3 were waited for; matrix products, arithmetic and copies ran while one was open for 7% of the time, Pallas kernels for 0%

profile of v1, /device:TPU:0, one launch (start us, length us, event | category | flops | bytes accessed | tf_op | source)
XLA Modules:
  0.0 56.4 jit_solution(7099159384975830834)
XLA Ops:
  0.0 1.4 %fusion.38 = (f32[2,4,16]{2,1,0:T(4,128)S(1)}, f32[2,4,16,128]{3,2,1,0:T(8,128)S(1)}) fusion(bf16[2,4,16,128]{3,2,1,0:T(8,128)(2,1)} %bitcast.83, bf16[2,128,512]{2,1,0:T(8,128)(2,1)} %param.12), kind=kOutput, calls=%fused_computation.47 | convolution fusion | flops 4226944 | bytes 360960 | tf_op jit(solution)/shard_map/sgjd,scgd->sgjc/dot_general | solution.py:39
  1.5 0.2 fusion.23
  2.0 1.2 %fusion.17 = f32[2,4,16,128]{3,2,1,0:T(8,128)S(1)} fusion(f32[2,4,16,128]{3,2,1,0:T(8,128)S(1)} %get-tuple-element.9, f32[2,4,16]{2,1,0:T(4,128)S(1)} %get-tuple-element.8, bf16[2,128,512]{2,1,0:T(8,128)(2,1)} %param.13), kind=kOutput, calls=%fused_computation.12 | convolution fusion | flops 4227072 | bytes 393728 | tf_op jit(solution)/shard_map/sgjc,scgd->sgjd/dot_general | solution.py:45
  3.4 0.7 %copy.69 = f32[32,1,520]{2,1,0:T(1,128)} copy(f32[32,1,520]{2,0,1:T(8,128)S(1)} %maximum_bitcast_fusion) | data formatting | bytes 133120 | tf_op jit(solution)/shard_map/all_to_all | solution.py:13
  4.1 7.3 %all-to-all-start = ((f32[32,1,520]{2,1,0:T(1,128)}), f32[32,1,520]{2,1,0:T(1,128)S(1)}, u32[]{:S(2)}, u32[]{:S(2)}) async-start(f32[32,1,520]{2,1,0:T(1,128)} %copy.69), calls=%async_computation | async-start | bytes 163840 | tf_op jit(solution)/shard_map/all_to_all | solution.py:13
  11.4 4.1 %copy.75 = bf16[4096,256]{1,0:T(8,128)(2,1)} copy(bf16[4096,256]{0,1:T(8,128)(2,1)} %bitcast.74) | data formatting | bytes 4194304 | tf_op jit(solution)/shard_map/dot_general | solution.py:73
  15.5 3.5 %all-to-all-done = f32[32,1,520]{2,1,0:T(1,128)S(1)} async-done(((f32[32,1,520]{2,1,0:T(1,128)}), f32[32,1,520]{2,1,0:T(1,128)S(1)}, u32[]{:S(2)}, u32[]{:S(2)}) %all-to-all-start) | async-done | bytes 66592 | tf_op jit(solution)/shard_map/all_to_all | solution.py:13
  19.0 0.1 copy.70
  19.1 0.1 fusion.37
  19.3 0.2 fusion.22
  19.5 0.2 multiply_reduce_fusion
  19.8 2.9 %convolution_bitcast_fusion = f32[32,2,128]{2,1,0:T(2,128)} fusion(bf16[2,256,1]{1,0,2:T(2,128)(2,1)S(1)} %reshape.90, bf16[32,128,256]{2,1,0:T(8,128)(2,1)} %bitcast.73), kind=kOutput, calls=%fused_computation.8 | convolution fusion | flops 4194304 | bytes 2130944 | tf_op jit(solution)/shard_map/dot_general | solution.py:73
  22.6 2.6 %all-to-all-start.1 = ((f32[32,2,128]{2,1,0:T(2,128)}), f32[32,2,128]{2,1,0:T(2,128)S(1)}, u32[]{:S(2)}, u32[]{:S(2)}) async-start(f32[32,2,128]{2,1,0:T(2,128)} %convolution_bitcast_fusion), calls=%async_computation.1 | async-start | bytes 65536 | tf_op jit(solution)/shard_map/all_to_all | solution.py:13
  25.2 7.2 %all-to-all-done.1 = f32[32,2,128]{2,1,0:T(2,128)S(1)} async-done(((f32[32,2,128]{2,1,0:T(2,128)}), f32[32,2,128]{2,1,0:T(2,128)S(1)}, u32[]{:S(2)}, u32[]{:S(2)}) %all-to-all-start.1) | async-done | bytes 32800 | tf_op jit(solution)/shard_map/all_to_all | solution.py:13
  32.5 0.7 %convert_add_fusion = f32[2,128]{1,0:T(2,128)S(1)} fusion(f32[2,128]{1,0:T(2,128)S(1)} %reduce_sum.66, bf16[2,4096]{1,0:T(2,128)(2,1)} %param.15, s32[]{:T(128)S(6)} %select_n.12), kind=kLoop, calls=%fused_computation.42 | loop fusion | flops 512 | bytes 2564 | tf_op jit(solution)/shard_map/add | solution.py:82
  33.1 0.6 %broadcast_in_dim.5 = f32[32,2,128]{2,1,0:T(2,128)} broadcast(f32[2,128]{1,0:T(2,128)S(1)} %convert_add_fusion), dimensions={1,2} | broadcast | bytes 33792 | tf_op jit(solution)/shard_map/broadcast_in_dim | solution.py:83
  33.8 2.6 %all-to-all-start.2 = ((f32[32,2,128]{2,1,0:T(2,128)}), f32[32,2,128]{2,1,0:T(2,128)S(1)}, u32[]{:S(2)}, u32[]{:S(2)}) async-start(f32[32,2,128]{2,1,0:T(2,128)} %broadcast_in_dim.5), calls=%async_computation.2 | async-start | bytes 65536 | tf_op jit(solution)/shard_map/all_to_all | solution.py:13
  36.4 0.1 fusion.34
  36.5 7.1 %all-to-all-done.2 = f32[32,2,128]{2,1,0:T(2,128)S(1)} async-done(((f32[32,2,128]{2,1,0:T(2,128)}), f32[32,2,128]{2,1,0:T(2,128)S(1)}, u32[]{:S(2)}, u32[]{:S(2)}) %all-to-all-start.2) | async-done | bytes 32800 | tf_op jit(solution)/shard_map/all_to_all | solution.py:13
  43.6 0.1 fusion.26
  43.7 0.5 fusion.4
  44.2 2.7 %fusion.6 = bf16[32,2,128]{2,1,0:T(2,128)(2,1)S(1)} fusion(bf16[1,192,4096]{2,1,0:T(8,128)(2,1)S(1)} %copy-done, bf16[1,4096,192]{1,2,0:T(8,128)(2,1)} %param.18, f32[2]{0:T(128)S(1)} %fusion.34, f32[2,192]{1,0:T(2,128)S(1)} %fusion.4, f32[32,2,128]{2,1,0:T(2,128)S(1)} %all-to-all-done.2, f32[2]{0:T(128)S(1)} %add_rsqrt_fusion, f32[32,128]{1,0:T(8,128)S(1)} %bitcast.82), kind=kOutput, calls=%fused_computation.9 | convolution fusion | flops 6334720 | bytes 3212816 | tf_op jit(solution)/shard_map/dot_general | solution.py:93
  46.9 8.9 %all_to_all.27 = bf16[32,2,128]{2,1,0:T(2,128)(2,1)S(1)} all-to-all(bf16[32,2,128]{2,1,0:T(2,128)(2,1)S(1)} %fusion.6), channel_id=1, replica_groups=mesh['group'=1,'ctx'=32] {'ctx'}, dimensions={0} | all-to-all | bytes 32768 | tf_op jit(solution)/shard_map/all_to_all | solution.py:13
  55.8 0.6 %add.26 = f32[2,128]{1,0:T(2,128)} add(f32[2,128]{1,0:T(2,128)S(1)} %convert_add_fusion, f32[2,128]{1,0:T(2,128)S(1)} %convert_reduce_fusion) | non-fusion elementwise | flops 256 | bytes 3072 | tf_op jit(solution)/shard_map/add | solution.py:96
  (28 shorter events, 0.8 us)
Async XLA Ops:
  0.0 44.2 %copy-start = (bf16[1,192,4096]{2,1,0:T(8,128)(2,1)S(1)}, bf16[1,192,4096]{2,1,0:T(8,128)(2,1)}, u32[]{:S(2)}) copy-start(bf16[1,192,4096]{2,1,0:T(8,128)(2,1)} %param.19) | copy-start | bytes 4718596
  4.1 14.9 %all-to-all-start = ((f32[32,1,520]{2,1,0:T(1,128)}), f32[32,1,520]{2,1,0:T(1,128)S(1)}, u32[]{:S(2)}, u32[]{:S(2)}) async-start(f32[32,1,520]{2,1,0:T(1,128)} %copy.69), calls=%async_computation | async-start | bytes 163840 | tf_op jit(solution)/shard_map/all_to_all | solution.py:13
  15.5 20.8 %copy-start.3 = (f32[2,4]{1,0:T(2,128)S(1)}, f32[2,4]{1,0:T(2,128)}, u32[]{:S(2)}) copy-start(f32[2,4]{1,0:T(2,128)} %param.21) | copy-start | bytes 100
  15.5 20.8 %copy-start.4 = (s32[2,4]{1,0:T(2,128)S(1)}, s32[2,4]{1,0:T(2,128)}, u32[]{:S(2)}) copy-start(s32[2,4]{1,0:T(2,128)} %param.20) | copy-start | bytes 100
  15.5 28.2 %copy-start.1 = (bf16[1,4096,192]{1,2,0:T(8,128)(2,1)S(1)}, bf16[1,4096,192]{1,2,0:T(8,128)(2,1)}, u32[]{:S(2)}) copy-start(bf16[1,4096,192]{1,2,0:T(8,128)(2,1)} %param.17) | copy-start | bytes 4718596
  15.5 28.2 %copy-start.2 = (f32[4096]{0:T(1024)S(1)}, f32[4096]{0:T(1024)}, u32[]{:S(2)}) copy-start(f32[4096]{0:T(1024)} %param.16) | copy-start | bytes 49156
  22.6 9.8 %all-to-all-start.1 = ((f32[32,2,128]{2,1,0:T(2,128)}), f32[32,2,128]{2,1,0:T(2,128)S(1)}, u32[]{:S(2)}, u32[]{:S(2)}) async-start(f32[32,2,128]{2,1,0:T(2,128)} %convolution_bitcast_fusion), calls=%async_computation.1 | async-start | bytes 65536 | tf_op jit(solution)/shard_map/all_to_all | solution.py:13
  33.8 9.8 %all-to-all-start.2 = ((f32[32,2,128]{2,1,0:T(2,128)}), f32[32,2,128]{2,1,0:T(2,128)S(1)}, u32[]{:S(2)}, u32[]{:S(2)}) async-start(f32[32,2,128]{2,1,0:T(2,128)} %broadcast_in_dim.5), calls=%async_computation.2 | async-start | bytes 65536 | tf_op jit(solution)/shard_map/all_to_all | solution.py:13

commit v2 on v1

v2 whole, which is shorter than its diff:
```python
import functools

import jax
import jax.numpy as jnp
from jax import lax
from jax.experimental import pallas as pl
from jax.experimental.pallas import tpu as pltpu
from jax.sharding import PartitionSpec as P

QUARTERS = 8


eps = 1e-06
LIMIT = 16 << 20
LONG = 1 << 34
f32 = jnp.float32
bf16 = jnp.bfloat16


def in_vmem(array):
    return pltpu.with_memory_space_constraint(array, pltpu.VMEM)


def in_hbm(array):
    return pltpu.with_memory_space_constraint(array, pltpu.HBM)


def call(kernel, out_shape, in_specs=None, count=0, scratch=(), flops=1 << 10, moved=1 << 10):
    vmem = pl.BlockSpec(memory_space=pltpu.VMEM)
    many = isinstance(out_shape, (tuple, list))
    return pl.pallas_call(
        kernel,
        out_shape=out_shape,
        in_specs=in_specs or [vmem] * count,
        out_specs=[vmem] * len(out_shape) if many else vmem,
        scratch_shapes=list(scratch),
        compiler_params=pltpu.CompilerParams(vmem_limit_bytes=LIMIT),
        cost_estimate=pl.CostEstimate(flops=flops, bytes_accessed=moved, transcendentals=0),
    )


def dot_nt(a, b):
    return lax.dot_general(a, b, (((1,), (1,)), ((), ())), preferred_element_type=f32)


def attend_kernel(heads_dev, kv_heads, q_hbm, k_hbm, v_hbm, out_ref, q, k, v, sems):
    seq_count, local_len, _ = k.shape
    head_dim = q.shape[1]
    head_count = q.shape[0] // seq_count
    copies = [
        pltpu.make_async_copy(src, dst, sems.at[n])
        for n, (src, dst) in enumerate(((q_hbm, q), (k_hbm, k), (v_hbm, v)))
    ]
    for copy in copies:
        copy.start()
    half = seq_count * heads_dev
    owners = head_count // kv_heads // heads_dev
    rows = owners * 2 * half
    row = lax.broadcasted_iota(jnp.int32, (rows, 1), 0)
    within = lax.rem(row, half)
    seq_of = lax.rem(within, seq_count)
    head_of = lax.div(row, 2 * half) * heads_dev + lax.div(within, seq_count)
    source = seq_of * head_count + head_of
    column = lax.broadcasted_iota(jnp.int32, (rows, q.shape[0]), 1)
    is_part = lax.rem(row, 2 * half) < half
    lane = lax.broadcasted_iota(jnp.int32, (rows, head_dim), 1)
    copies[0].wait()
    copies[1].wait()
    numers = []
    stats = []
    for g in range(kv_heads):
        pick = jnp.where(column == source + g * owners * heads_dev, 1.0, 0.0).astype(bf16)
        picked = jnp.dot(pick, q[...], preferred_element_type=f32).astype(bf16)
        feats = slice(g * head_dim, (g + 1) * head_dim)
        scores = dot_nt(picked, k[0, :, feats])
        for s in range(1, seq_count):
            scores = jnp.where(seq_of == s, dot_nt(picked, k[s, :, feats]), scores)
        scores = scores * head_dim ** (-0.5)
        peak = jnp.max(scores, axis=1, keepdims=True)
        numer = jnp.exp(scores - peak)
        denom = jnp.sum(numer, axis=1, keepdims=True)
        numers.append(numer.astype(bf16))
        stats.append(jnp.where(lane < head_dim // 2, peak, denom))
    copies[2].wait()
    for g in range(kv_heads):
        feats = slice(g * head_dim, (g + 1) * head_dim)
        part = jnp.dot(numers[g], v[0, :, feats], preferred_element_type=f32)
        for s in range(1, seq_count):
            other = jnp.dot(numers[g], v[s, :, feats], preferred_element_type=f32)
            part = jnp.where(seq_of == s, other, part)
        block = jnp.where(is_part, part, stats[g])
        out_ref[g * owners : (g + 1) * owners] = block.reshape(owners, 2 * half, head_dim)


def attend(queries, key_cache, value_cache, devices, heads_dev):
    seq_count, head_count, head_dim = queries.shape
    hbm = pl.BlockSpec(memory_space=pltpu.HBM)
    q = in_hbm(queries.reshape(seq_count * head_count, head_dim))
    kernel = functools.partial(attend_kernel, heads_dev, key_cache.shape[2] // head_dim)
    return call(
        kernel,
        jax.ShapeDtypeStruct((devices, 2 * seq_count * heads_dev, head_dim), f32),
        in_specs=[hbm] * 3,
        scratch=(
            pltpu.VMEM(q.shape, bf16),
            pltpu.VMEM(key_cache.shape, bf16),
            pltpu.VMEM(value_cache.shape, bf16),
            pltpu.SemaphoreType.DMA((3,)),
        ),
        flops=LONG,
    )(q, in_hbm(key_cache), in_hbm(value_cache))


def project_kernel(seq_count, got_ref, weight_ref, send_ref, keep_ref):
    core = lax.rem(lax.axis_index("ctx"), 2)
    head_dim = got_ref.shape[2]
    half = got_ref.shape[1] // 2
    stats = got_ref[:, half:, :]
    peaks = stats[:, :, 0:1]
    scale = jnp.exp(peaks - jnp.max(peaks, axis=0, keepdims=True))
    denoms = jnp.sum(scale * stats[:, :, head_dim // 2 : head_dim // 2 + 1], axis=0)
    summed = jnp.sum(scale * got_ref[:, :half, :], axis=0)
    attended = (summed / denoms).astype(bf16)
    attended = jnp.concatenate(
        [attended[n : n + seq_count] for n in range(0, half, seq_count)], axis=1
    )
    mid = weight_ref.shape[1] // 2
    low = jnp.dot(attended, weight_ref[:, :mid], preferred_element_type=f32)
    high = jnp.dot(attended, weight_ref[:, mid:], preferred_element_type=f32)
    send_ref[...] = jnp.where(core == 0, high, low)
    keep_ref[...] = jnp.where(core == 0, low, high)


def spread_kernel(keep_ref, came_ref, out_ref):
    total = (keep_ref[...] + came_ref[...]).astype(out_ref.dtype)
    for n in range(out_ref.shape[0]):
        out_ref[n] = total


def resid_kernel(got_ref, hidden_ref, out_ref):
    core = lax.rem(lax.axis_index("ctx"), 2)
    mid = out_ref.shape[1]
    hidden = jnp.where(core == 0, hidden_ref[:, :mid].astype(f32), hidden_ref[:, mid:].astype(f32))
    total = got_ref[0].astype(f32)
    for n in range(1, got_ref.shape[0]):
        total = total + got_ref[n].astype(f32)
    out_ref[...] = hidden + total


def expert_kernel(
    mine_ref, came_ref, gain_ref, gate_ref, up_ref, down_ref, routes_ref, share_ref, out_ref, mine_out, resid_ref
):
    index = lax.axis_index("ctx")
    core = lax.rem(index, 2)
    expert = lax.div(index, QUARTERS)
    mid = mine_ref.shape[1]
    low = jnp.where(core == 0, mine_ref[...], came_ref[...])
    high = jnp.where(core == 0, came_ref[...], mine_ref[...])
    resid_ref[:, :mid] = low
    resid_ref[:, mid:] = high
    col_dev = mine_out.shape[1]
    if col_dev == 2 * mid:
        mine_out[...] = resid_ref[...]
    else:
        start = pl.multiple_of(index * col_dev, col_dev)
        mine_out[...] = resid_ref[:, pl.ds(start, col_dev)]
    square = jnp.sum(low * low, axis=1, keepdims=True) + jnp.sum(high * high, axis=1, keepdims=True)
    inverse_rms = lax.rsqrt(square / (2 * mid) + eps)
    low = (low * inverse_rms * gain_ref[:, :mid]).astype(bf16)
    high = (high * inverse_rms * gain_ref[:, mid:]).astype(bf16)
    gate_act = dot_nt(low, gate_ref[:, :mid]) + dot_nt(high, gate_ref[:, mid:])
    up_act = dot_nt(low, up_ref[:, :mid]) + dot_nt(high, up_ref[:, mid:])
    hidden = (gate_act / (1.0 + jnp.exp(-gate_act)) * up_act).astype(bf16)
    share = jnp.where(routes_ref[...] == expert, share_ref[...], 0.0)
    share = jnp.sum(share, axis=1, keepdims=True)
    out = jnp.dot(hidden, down_ref[...], preferred_element_type=f32)
    out_ref[...] = (out * share).astype(bf16)


def merge_parts(queries, key_cache, value_cache, devices):
    seq_count, head_count, head_dim = queries.shape
    kv_heads = key_cache.shape[2] // head_dim
    local_len = key_cache.shape[1]
    query_view = queries.reshape(seq_count, kv_heads, head_count // kv_heads, head_dim)
    key_view = key_cache.reshape(seq_count, local_len, kv_heads, head_dim)
    value_view = value_cache.reshape(seq_count, local_len, kv_heads, head_dim)
    scores = jnp.einsum(
        "sgjd,scgd->sgjc", query_view, key_view, preferred_element_type=f32
    ) * head_dim ** (-0.5)
    peak = jnp.max(scores, axis=-1)
    numer = jnp.exp(scores - peak[..., None])
    denom = jnp.sum(numer, axis=-1)
    weighted = jnp.einsum(
        "sgjc,scgd->sgjd", numer.astype(bf16), value_view, preferred_element_type=f32
    )
    width = head_count * head_dim // devices
    spread = head_dim // width

    def by_owner(stat):
        return jnp.repeat(stat.reshape(seq_count, head_count), spread, axis=1).T[..., None]

    weighted = weighted.reshape(seq_count, devices, width).transpose(1, 0, 2)
    sent = jnp.concatenate([weighted, by_owner(peak), by_owner(denom)], axis=2)
    got = swap_blocks(sent)
    peaks = got[:, :, width : width + 1]
    scale = jnp.exp(peaks - jnp.max(peaks, axis=0))
    denoms = jnp.sum(scale * got[:, :, width + 1 :], axis=0)
    return (jnp.sum(scale * got[:, :, :width], axis=0) / denoms).astype(bf16)


def swap_blocks(blocks, groups=None):
    return lax.all_to_all(
        blocks, "ctx", split_axis=0, concat_axis=0, tiled=True, axis_index_groups=groups
    )


def body(
    queries,
    key_cache,
    value_cache,
    out_weight,
    hidden_in,
    norm_gain,
    gate_weight,
    up_weight,
    down_weight,
    routes,
    route_weight,
):
    devices = lax.axis_size("ctx")
    my_index = lax.axis_index("ctx")
    seq_count, head_count, head_dim = queries.shape
    model_width = hidden_in.shape[1]
    mid = model_width // 2
    feat_dev = head_count * head_dim // devices
    half = jax.ShapeDtypeStruct((seq_count, mid), f32)
    if feat_dev % head_dim == 0:
        heads_dev = feat_dev // head_dim
        got = swap_blocks(attend(queries, key_cache, value_cache, devices, heads_dev))
        send, keep = call(functools.partial(project_kernel, seq_count), (half, half), count=2)(
            got, in_vmem(out_weight)
        )
    else:
        attended = merge_parts(queries, key_cache, value_cache, devices)
        proj = jnp.dot(attended, out_weight, preferred_element_type=f32)
        low, high = proj[:, :mid], proj[:, mid:]
        first = lax.rem(my_index, 2) == 0
        send, keep = jnp.where(first, high, low), jnp.where(first, low, high)
    pairs = [(n, n ^ 1) for n in range(devices)]
    chips = devices // 2
    groups = [[2 * n + core for n in range(chips)] for core in range(2)]
    came = lax.ppermute(send, "ctx", pairs)
    spread = call(spread_kernel, jax.ShapeDtypeStruct((chips, seq_count, mid), bf16), count=2, flops=LONG)(
        keep, came
    )
    mine = call(resid_kernel, half, count=2)(swap_blocks(spread, groups), hidden_in)
    came = lax.ppermute(mine, "ctx", pairs)
    col_dev = model_width // devices
    aligned = col_dev % 128 == 0
    out, resid_mine = call(
        expert_kernel,
        (
            jax.ShapeDtypeStruct((seq_count, model_width), bf16),
            jax.ShapeDtypeStruct((seq_count, col_dev if aligned else model_width), f32),
        ),
        count=8,
        scratch=(pltpu.VMEM((seq_count, model_width), f32),),
    )(
        mine,
        came,
        norm_gain.reshape(1, model_width),
        in_vmem(gate_weight[0].T),
        in_vmem(up_weight[0].T),
        in_vmem(down_weight[0]),
        routes,
        route_weight,
    )
    blocks = lax.all_to_all(
        out.reshape(seq_count, devices, col_dev), "ctx", split_axis=1, concat_axis=1, tiled=True
    )
    if not aligned:
        resid_mine = lax.dynamic_slice_in_dim(resid_mine, my_index * col_dev, col_dev, 1)
    return resid_mine + jnp.sum(blocks.astype(f32), axis=1)


def solution(mesh):
    in_specs = (
        P("group", None, None),
        P("group", "ctx", None),
        P("group", "ctx", None),
        P("ctx", None),
        P("group", None),
        P(),
        P("ctx", None, None),
        P("ctx", None, None),
        P("ctx", None, None),
        P("group", None),
        P("group", None),
    )
    out_specs = P("group", "ctx")
    return jax.shard_map(body, mesh=mesh, in_specs=in_specs, out_specs=out_specs, check_vma=False)
```

time: 56.8 us -> 42.9 us (0.76)
  blocking collectives: 8.87 us -> 35.4 us
  waiting for transfers between devices: 17.8 us -> 2.14 us
  starting transfers between devices: 12.5 us -> 0.32 us
  matrix products: 8.62 us -> 0 us
  local copies, waits for them, and re-layouts: 6.21 us -> 0.04 us
  Pallas kernels: 0 us -> 4.09 us
  other arithmetic: 2.26 us -> 0.61 us
    all_to_all x1 -> x3, blocking collectives: 8.87 us -> 35.4 us  [the longest x2 26.3 us: swap_blocks(): lax.all_to_all(blocks, 'ctx', split_axis=0, concat_axis=0, tiled=True, ax...]
    all_to_all x3 -> x0, waiting for transfers between devices: 17.8 us -> none  [swap_blocks(): lax.all_to_all(blocks, 'ctx', split_axis=0, concat_axis=0, tiled=True)]
    all_to_all x3 -> x0, starting transfers between devices: 12.5 us -> none  [swap_blocks(): lax.all_to_all(blocks, 'ctx', split_axis=0, concat_axis=0, tiled=True)]
    dot_general x5 -> x0, matrix products: 8.62 us -> none  [the longest x1 2.85 us: body(): jnp.dot(attended, out_weight, preferred_element_type=jnp.float32)]
    dot_general x1 -> x0, local copies, waits for them, and re-layouts: 4.11 us -> none  [body(): jnp.dot(attended, out_weight, preferred_element_type=jnp.float32)]
    pallas_call x0 -> x5, Pallas kernels: none -> 4.09 us  [the longest x1 2.19 us: attend(): call(kernel, jax.ShapeDtypeStruct((devices, 2 * seq_count * heads_dev, he...]
    ppermute x0 -> x2, waiting for transfers between devices: none -> 2.14 us  [the longest x1 1.17 us: body(): came = lax.ppermute(mine, 'ctx', pairs)]
    all_to_all x2 -> x0, local copies, waits for them, and re-layouts: 0.86 us -> none  [swap_blocks(): lax.all_to_all(blocks, 'ctx', split_axis=0, concat_axis=0, tiled=True)]
  transfers between devices with their start and end apart: 3 -> 2, of which waited for: 3 -> 2; matrix products, arithmetic and copies ran while one was open for 7% -> 0% of each run, Pallas kernels for 0% -> 0%
where the time goes in v2:
time: 42.9 us; the launch traced here: 42.6 us
  blocking collectives  35.4 us (83%)
  Pallas kernels  4.09 us (10%)
  waiting for transfers between devices  2.14 us (5%)
  other arithmetic  0.61 us (1%)
    all_to_all x2, blocking collectives, swap_blocks(): lax.all_to_all(blocks, 'ctx', split_axis=0, concat_axis=0, tiled=True, ax...  26.3 us
    all_to_all x1, blocking collectives, body(): lax.all_to_all(out.reshape(seq_count, devices, col_dev), 'ctx', split_axi...  9.07 us
    pallas_call x1, Pallas kernels, attend(): call(kernel, jax.ShapeDtypeStruct((devices, 2 * seq_count * heads_dev, he...  2.19 us
    pallas_call x1, Pallas kernels, body(): call(expert_kernel, (jax.ShapeDtypeStruct((seq_count, model_width), bf16)...  1.32 us
    ppermute x1, waiting for transfers between devices, body(): came = lax.ppermute(mine, 'ctx', pairs)  1.17 us
    ppermute x1, waiting for transfers between devices, body(): came = lax.ppermute(send, 'ctx', pairs)  0.97 us
  transfers between devices with their start and end apart: 2, of which 2 were waited for; matrix products, arithmetic and copies ran while one was open for 0% of the time, Pallas kernels for 0%

profile of v2, /device:TPU:0, one launch (start us, length us, event | category | flops | bytes accessed | tf_op | source)
XLA Modules:
  0.0 42.6 jit_solution(2778440533324361371)
XLA Ops:
  0.0 0.0 copy-start
  0.0 2.2 %shard_map.109 = f32[32,8,128]{2,1,0:T(8,128)S(1)} custom-call(bf16[128,128]{1,0:T(8,128)(2,1)} %bitcast.15, bf16[2,128,512]{2,1,0:T(8,128)(2,1)} %k_hbm.1, bf16[2,128,512]{2,1,0:T(8,128)(2,1)} %v_hbm.1), custom_call_target="tpu_custom_call" | custom-call | flops 17179869184 | bytes 1024 | tf_op jit(solution)/shard_map/pallas_call | solution.py:100
  2.2 15.3 %all_to_all.15.got_ref = f32[32,8,128]{2,1,0:T(8,128)S(1)} all-to-all(f32[32,8,128]{2,1,0:T(8,128)S(1)} %shard_map.109), channel_id=1, replica_groups=mesh['group'=1,'ctx'=32] {'ctx'}, dimensions={0} | all-to-all | bytes 262144 | tf_op jit(solution)/shard_map/all_to_all | solution.py:212
  17.5 0.0 copy-done
  17.5 0.5 %shard_map.110 = (f32[2,2048]{1,0:T(2,128)S(1)}, f32[2,2048]{1,0:T(2,128)S(1)}) custom-call(f32[32,8,128]{2,1,0:T(8,128)S(1)} %all_to_all.15.got_ref, bf16[256,4096]{1,0:T(8,128)(2,1)S(1)} %copy-done), custom_call_target="tpu_custom_call" | custom-call | flops 1024 | bytes 1024 | tf_op jit(solution)/shard_map/pallas_call | solution.py:240
  18.1 0.3 collective-permute-start
  18.3 1.0 %collective-permute-done.came_ref = f32[2,2048]{1,0:T(2,128)S(1)} collective-permute-done((f32[2,2048]{1,0:T(2,128)S(1)}, f32[2,2048]{1,0:T(2,128)S(1)}, u32[]{:S(2)}, u32[]{:S(2)}) %collective-permute-start) | collective-permute-done | bytes 16416 | tf_op jit(solution)/shard_map/ppermute | solution.py:252
  19.3 0.0 copy-start.5
  19.3 0.0 copy-start.4
  19.3 0.0 copy-start.6
  19.3 0.0 copy-start.7
  19.4 11.0 %all_to_all.16.got_ref = bf16[16,2,2048]{2,1,0:T(2,128)(2,1)S(1)} all-to-all(bf16[16,2,2048]{2,1,0:T(2,128)(2,1)S(1)} %shard_map.111), channel_id=1, replica_groups={{0,2,4,6,8,10,12,14,16,18,20,22,24,26,28,30},{1,3,5,7,9,11,13,15,17,19,..., dimensions={0} | all-to-all | bytes 262144 | tf_op jit(solution)/shard_map/all_to_all | solution.py:212
  30.3 0.0 copy-done.5
  30.4 0.1 collective-permute-start.1
  30.4 1.2 %collective-permute-done.1.came_ref = f32[2,2048]{1,0:T(2,128)S(1)} collective-permute-done((f32[2,2048]{1,0:T(2,128)S(1)}, f32[2,2048]{1,0:T(2,128)S(1)}, u32[]{:S(2)}, u32[]{:S(2)}) %collective-permute-start.1) | collective-permute-done | bytes 16416 | tf_op jit(solution)/shard_map/ppermute | solution.py:257
  31.6 0.0 copy-done.1
  31.6 0.0 copy-done.2
  31.6 0.0 copy-done.3
  31.6 0.0 copy-done.4
  31.6 0.0 copy-done.6
  31.6 0.0 copy-done.7
  31.6 1.3 %shard_map.113 = (bf16[2,4096]{1,0:T(2,128)(2,1)S(1)}, f32[2,128]{1,0:T(2,128)S(1)}) custom-call(f32[2,2048]{1,0:T(2,128)S(1)} %shard_map.112.mine_ref, f32[2,2048]{1,0:T(2,128)S(1)} %collective-permute-done.1.came_ref, f32[1,4096]{1,0:T(1,128)S(1)} %bitcast.13, bf16[192,4096]{1,0:T(8,128)(2,1)S(1)} %bitcast.10, bf16[192,4096]{1,0:T(8,128)(2,1)S(1)} %bitcast.11, ...), custom_call_target="tpu_custom_call" | custom-call | flops 1024 | bytes 1024 | tf_op jit(solution)/shard_map/pallas_call | solution.py:260
  33.0 9.1 %all_to_all.17 = bf16[2,32,128]{2,0,1:T(2,128)(2,1)S(1)} all-to-all(bf16[2,32,128]{2,0,1:T(2,128)(2,1)S(1)} %bitcast.14), channel_id=1, replica_groups=mesh['group'=1,'ctx'=32] {'ctx'}, dimensions={1} | all-to-all | bytes 32768 | tf_op jit(solution)/shard_map/all_to_all | solution.py:278
  42.1 0.6 %add.3 = f32[2,128]{1,0:T(2,128)} add(f32[2,128]{1,0:T(2,128)S(1)} %get-tuple-element.11, f32[2,128]{1,0:T(2,128)S(1)} %convert_reduce_fusion) | non-fusion elementwise | flops 256 | bytes 3072 | tf_op jit(solution)/shard_map/add | solution.py:283
  (6 shorter events, 0.1 us)
Async XLA Ops:
  0.0 17.5 %copy-start = (bf16[256,4096]{1,0:T(8,128)(2,1)S(1)}, bf16[256,4096]{1,0:T(8,128)(2,1)}, u32[]{:S(2)}) copy-start(bf16[256,4096]{1,0:T(8,128)(2,1)} %weight_ref.1) | copy-start | bytes 6291460
  18.1 1.2 %collective-permute-start = (f32[2,2048]{1,0:T(2,128)S(1)}, f32[2,2048]{1,0:T(2,128)S(1)}, u32[]{:S(2)}, u32[]{:S(2)}) collective-permute-start(f32[2,2048]{1,0:T(2,128)S(1)} %get-tuple-element.10), channel_id=1, source_target_pairs={{0,1},{1,0},{2,3},{3,2},{4,5},{5,4},{6,7},{7,6},{8,9},{9,8},{10,11... | collective-permute-start | bytes 49160 | tf_op jit(solution)/shard_map/ppermute | solution.py:252
  19.3 11.0 %copy-start.5 = (bf16[2,4096]{1,0:T(2,128)(2,1)S(1)}, bf16[2,4096]{1,0:T(2,128)(2,1)}, u32[]{:S(2)}) copy-start(bf16[2,4096]{1,0:T(2,128)(2,1)} %hidden_ref.1) | copy-start | bytes 49156
  19.3 12.3 %copy-start.1 = (bf16[1,4096,192]{1,2,0:T(8,128)(2,1)S(1)}, bf16[1,4096,192]{1,2,0:T(8,128)(2,1)}, u32[]{:S(2)}) copy-start(bf16[1,4096,192]{1,2,0:T(8,128)(2,1)} %param.17) | copy-start | bytes 4718596
  19.3 12.3 %copy-start.2 = (bf16[1,4096,192]{1,2,0:T(8,128)(2,1)S(1)}, bf16[1,4096,192]{1,2,0:T(8,128)(2,1)}, u32[]{:S(2)}) copy-start(bf16[1,4096,192]{1,2,0:T(8,128)(2,1)} %param.18) | copy-start | bytes 4718596
  19.3 12.3 %copy-start.3 = (bf16[1,192,4096]{2,1,0:T(8,128)(2,1)S(1)}, bf16[1,192,4096]{2,1,0:T(8,128)(2,1)}, u32[]{:S(2)}) copy-start(bf16[1,192,4096]{2,1,0:T(8,128)(2,1)} %param.19) | copy-start | bytes 4718596
  19.3 12.3 %copy-start.4 = (f32[4096]{0:T(1024)S(1)}, f32[4096]{0:T(1024)}, u32[]{:S(2)}) copy-start(f32[4096]{0:T(1024)} %param.16) | copy-start | bytes 49156
  19.3 12.3 %copy-start.6 = (s32[2,4]{1,0:T(2,128)S(1)}, s32[2,4]{1,0:T(2,128)}, u32[]{:S(2)}) copy-start(s32[2,4]{1,0:T(2,128)} %routes_ref.1) | copy-start | bytes 100
  19.3 12.3 %copy-start.7 = (f32[2,4]{1,0:T(2,128)S(1)}, f32[2,4]{1,0:T(2,128)}, u32[]{:S(2)}) copy-start(f32[2,4]{1,0:T(2,128)} %share_ref.1) | copy-start | bytes 100
  30.4 1.2 %collective-permute-start.1 = (f32[2,2048]{1,0:T(2,128)S(1)}, f32[2,2048]{1,0:T(2,128)S(1)}, u32[]{:S(2)}, u32[]{:S(2)}) collective-permute-start(f32[2,2048]{1,0:T(2,128)S(1)} %shard_map.112.mine_ref), channel_id=1, source_target_pairs={{0,1},{1,0},{2,3},{3,2},{4,5},{5,4},{6,7},{7,6},{8,9},{9,8},{10,11... | collective-permute-start | bytes 49160 | tf_op jit(solution)/shard_map/ppermute | solution.py:257

commit v3 on v2

--- a/solution.py
+++ b/solution.py
@@ -43,14 +43,12 @@
     return lax.dot_general(a, b, (((1,), (1,)), ((), ())), preferred_element_type=f32)
 
 
-def attend_kernel(heads_dev, kv_heads, q_hbm, k_hbm, v_hbm, out_ref, q, k, v, sems):
+def attend_kernel(heads_dev, kv_heads, q_hbm, k_hbm, v_hbm, w_hbm, out_ref, w_ref, q, k, v, sems):
     seq_count, local_len, _ = k.shape
     head_dim = q.shape[1]
     head_count = q.shape[0] // seq_count
-    copies = [
-        pltpu.make_async_copy(src, dst, sems.at[n])
-        for n, (src, dst) in enumerate(((q_hbm, q), (k_hbm, k), (v_hbm, v)))
-    ]
+    moves = ((q_hbm, q), (k_hbm, k), (v_hbm, v), (w_hbm, w_ref))
+    copies = [pltpu.make_async_copy(src, dst, sems.at[n]) for n, (src, dst) in enumerate(moves)]
     for copy in copies:
         copy.start()
     half = seq_count * heads_dev
@@ -62,64 +60,80 @@
     head_of = lax.div(row, 2 * half) * heads_dev + lax.div(within, seq_count)
     source = seq_of * head_count + head_of
     column = lax.broadcasted_iota(jnp.int32, (rows, q.shape[0]), 1)
+    picks = [
+        jnp.where(column == source + g * owners * heads_dev, 1.0, 0.0).astype(bf16)
+        for g in range(kv_heads)
+    ]
     is_part = lax.rem(row, 2 * half) < half
     lane = lax.broadcasted_iota(jnp.int32, (rows, head_dim), 1)
+    third = head_dim // 3
+
+    def by_seq(values):
+        return jnp.concatenate(
+            [jnp.where(seq_of == s, values, 0.0).astype(bf16) for s in range(seq_count)], axis=1
+        )
+
     copies[0].wait()
+    queries = [by_seq(jnp.dot(pick, q[...], preferred_element_type=f32)) for pick in picks]
     copies[1].wait()
+    feats = [slice(g * head_dim, (g + 1) * head_dim) for g in range(kv_heads)]
+    scores = [
+        dot_nt(queries[g], jnp.concatenate([k[s, :, feats[g]] for s in range(seq_count)], axis=1))
+        * head_dim ** (-0.5)
+        for g in range(kv_heads)
+    ]
     numers = []
     stats = []
     for g in range(kv_heads):
-        pick = jnp.where(column == source + g * owners * heads_dev, 1.0, 0.0).astype(bf16)
-        picked = jnp.dot(pick, q[...], preferred_element_type=f32).astype(bf16)
-        feats = slice(g * head_dim, (g + 1) * head_dim)
-        scores = dot_nt(picked, k[0, :, feats])
-        for s in range(1, seq_count):
-            scores = jnp.where(seq_of == s, dot_nt(picked, k[s, :, feats]), scores)
-        scores = scores * head_dim ** (-0.5)
-        peak = jnp.max(scores, axis=1, keepdims=True)
-        numer = jnp.exp(scores - peak)
+        peak = jnp.max(scores[g], axis=1, keepdims=True).astype(bf16).astype(f32)
+        numer = jnp.exp(scores[g] - peak)
         denom = jnp.sum(numer, axis=1, keepdims=True)
-        numers.append(numer.astype(bf16))
-        stats.append(jnp.where(lane < head_dim // 2, peak, denom))
+        coarse = denom.astype(bf16).astype(f32)
+        totals = jnp.where(lane < 2 * third, coarse, denom - coarse)
+        stats.append(jnp.where(lane < third, peak, totals))
+        numers.append(by_seq(numer))
     copies[2].wait()
     for g in range(kv_heads):
-        feats = slice(g * head_dim, (g + 1) * head_dim)
-        part = jnp.dot(numers[g], v[0, :, feats], preferred_element_type=f32)
-        for s in range(1, seq_count):
-            other = jnp.dot(numers[g], v[s, :, feats], preferred_element_type=f32)
-            part = jnp.where(seq_of == s, other, part)
-        block = jnp.where(is_part, part, stats[g])
+        values = jnp.concatenate([v[s, :, feats[g]] for s in range(seq_count)], axis=0)
+        part = jnp.dot(numers[g], values, preferred_element_type=f32)
+        block = jnp.where(is_part, part, stats[g]).astype(bf16)
         out_ref[g * owners : (g + 1) * owners] = block.reshape(owners, 2 * half, head_dim)
-
-
-def attend(queries, key_cache, value_cache, devices, heads_dev):
+    copies[3].wait()
+
+
+def attend(queries, key_cache, value_cache, out_weight, devices, heads_dev):
     seq_count, head_count, head_dim = queries.shape
     hbm = pl.BlockSpec(memory_space=pltpu.HBM)
-    q = in_hbm(queries.reshape(seq_count * head_count, head_dim))
+    q = queries.reshape(seq_count * head_count, head_dim)
     kernel = functools.partial(attend_kernel, heads_dev, key_cache.shape[2] // head_dim)
     return call(
         kernel,
-        jax.ShapeDtypeStruct((devices, 2 * seq_count * heads_dev, head_dim), f32),
-        in_specs=[hbm] * 3,
+        (
+            pltpu.VMEM((devices, 2 * seq_count * heads_dev, head_dim), bf16),
+            pltpu.VMEM(out_weight.shape, bf16),
+        ),
+        in_specs=[hbm] * 4,
         scratch=(
             pltpu.VMEM(q.shape, bf16),
             pltpu.VMEM(key_cache.shape, bf16),
             pltpu.VMEM(value_cache.shape, bf16),
-            pltpu.SemaphoreType.DMA((3,)),
+            pltpu.SemaphoreType.DMA((4,)),
         ),
-        flops=LONG,
-    )(q, in_hbm(key_cache), in_hbm(value_cache))
+    )(in_hbm(q), in_hbm(key_cache), in_hbm(value_cache), in_hbm(out_weight))
 
 
 def project_kernel(seq_count, got_ref, weight_ref, send_ref, keep_ref):
     core = lax.rem(lax.axis_index("ctx"), 2)
     head_dim = got_ref.shape[2]
     half = got_ref.shape[1] // 2
-    stats = got_ref[:, half:, :]
+    got = got_ref[...].astype(f32)
+    third = head_dim // 3
+    stats = got[:, half:, :]
     peaks = stats[:, :, 0:1]
     scale = jnp.exp(peaks - jnp.max(peaks, axis=0, keepdims=True))
-    denoms = jnp.sum(scale * stats[:, :, head_dim // 2 : head_dim // 2 + 1], axis=0)
-    summed = jnp.sum(scale * got_ref[:, :half, :], axis=0)
+    total = stats[:, :, third : third + 1] + stats[:, :, 2 * third : 2 * third + 1]
+    denoms = jnp.sum(scale * total, axis=0)
+    summed = jnp.sum(scale * got[:, :half, :], axis=0)
     attended = (summed / denoms).astype(bf16)
     attended = jnp.concatenate(
         [attended[n : n + seq_count] for n in range(0, half, seq_count)], axis=1
@@ -133,18 +147,25 @@
 
 def spread_kernel(keep_ref, came_ref, out_ref):
     total = (keep_ref[...] + came_ref[...]).astype(out_ref.dtype)
+    quarter = out_ref.shape[2]
     for n in range(out_ref.shape[0]):
-        out_ref[n] = total
+        out_ref[n] = total[:, n % 2 * quarter : (n % 2 + 1) * quarter]
 
 
 def resid_kernel(got_ref, hidden_ref, out_ref):
     core = lax.rem(lax.axis_index("ctx"), 2)
-    mid = out_ref.shape[1]
-    hidden = jnp.where(core == 0, hidden_ref[:, :mid].astype(f32), hidden_ref[:, mid:].astype(f32))
-    total = got_ref[0].astype(f32)
-    for n in range(1, got_ref.shape[0]):
-        total = total + got_ref[n].astype(f32)
-    out_ref[...] = hidden + total
+    quarter = got_ref.shape[2]
+    for side in range(2):
+        start = 2 * side * quarter
+        hidden = jnp.where(
+            core == 0,
+            hidden_ref[:, start : start + quarter].astype(f32),
+            hidden_ref[:, start + quarter : start + 2 * quarter].astype(f32),
+        )
+        total = got_ref[side].astype(f32)
+        for n in range(side + 2, got_ref.shape[0], 2):
+            total = total + got_ref[n].astype(f32)
+        out_ref[:, side * quarter : (side + 1) * quarter] = hidden + total
 
 
 def expert_kernel(
@@ -154,8 +175,10 @@
     core = lax.rem(index, 2)
     expert = lax.div(index, QUARTERS)
     mid = mine_ref.shape[1]
-    low = jnp.where(core == 0, mine_ref[...], came_ref[...])
-    high = jnp.where(core == 0, came_ref[...], mine_ref[...])
+    even = jnp.where(core == 0, mine_ref[...], came_ref[...])
+    odd = jnp.where(core == 0, came_ref[...], mine_ref[...])
+    low = jnp.concatenate([even[:, : mid // 2], odd[:, : mid // 2]], axis=1)
+    high = jnp.concatenate([even[:, mid // 2 :], odd[:, mid // 2 :]], axis=1)
     resid_ref[:, :mid] = low
     resid_ref[:, mid:] = high
     col_dev = mine_out.shape[1]
@@ -208,10 +231,8 @@
     return (jnp.sum(scale * got[:, :, :width], axis=0) / denoms).astype(bf16)
 
 
-def swap_blocks(blocks, groups=None):
-    return lax.all_to_all(
-        blocks, "ctx", split_axis=0, concat_axis=0, tiled=True, axis_index_groups=groups
-    )
+def swap_blocks(blocks):
+    return lax.all_to_all(blocks, "ctx", split_axis=0, concat_axis=0, tiled=True)
 
 
 def body(
@@ -236,9 +257,9 @@
     half = jax.ShapeDtypeStruct((seq_count, mid), f32)
     if feat_dev % head_dim == 0:
         heads_dev = feat_dev // head_dim
-        got = swap_blocks(attend(queries, key_cache, value_cache, devices, heads_dev))
+        parts, weight = attend(queries, key_cache, value_cache, out_weight, devices, heads_dev)
         send, keep = call(functools.partial(project_kernel, seq_count), (half, half), count=2)(
-            got, in_vmem(out_weight)
+            swap_blocks(parts), weight
         )
     else:
         attended = merge_parts(queries, key_cache, value_cache, devices)
@@ -247,13 +268,14 @@
         first = lax.rem(my_index, 2) == 0
         send, keep = jnp.where(first, high, low), jnp.where(first, low, high)
     pairs = [(n, n ^ 1) for n in range(devices)]
-    chips = devices // 2
-    groups = [[2 * n + core for n in range(chips)] for core in range(2)]
     came = lax.ppermute(send, "ctx", pairs)
-    spread = call(spread_kernel, jax.ShapeDtypeStruct((chips, seq_count, mid), bf16), count=2, flops=LONG)(
-        keep, came
-    )
-    mine = call(resid_kernel, half, count=2)(swap_blocks(spread, groups), hidden_in)
+    spread = call(
+        spread_kernel,
+        jax.ShapeDtypeStruct((devices, seq_count, mid // 2), bf16),
+        count=2,
+        flops=LONG,
+    )(keep, came)
+    mine = call(resid_kernel, half, count=2)(swap_blocks(spread), hidden_in)
     came = lax.ppermute(mine, "ctx", pairs)
     col_dev = model_width // devices
     aligned = col_dev % 128 == 0

time: 42.9 us -> 40.8 us (0.951)
  blocking collectives: 35.4 us -> 33.6 us
    all_to_all x2, blocking collectives: 26.3 us -> 24.7 us  [swap_blocks(): lax.all_to_all(blocks, 'ctx', split_axis=0, concat_axis=0, tiled=True)]
where the time goes in v3:
time: 40.8 us; the launch traced here: 40.6 us
  blocking collectives  33.6 us (82%)
  Pallas kernels  3.79 us (9%)
  waiting for transfers between devices  2.04 us (5%)
  other arithmetic  0.61 us (1%)
  starting transfers between devices  0.43 us (1%)
    all_to_all x2, blocking collectives, swap_blocks(): lax.all_to_all(blocks, 'ctx', split_axis=0, concat_axis=0, tiled=True)  24.7 us
    all_to_all x1, blocking collectives, body(): lax.all_to_all(out.reshape(seq_count, devices, col_dev), 'ctx', split_axi...  8.87 us
    pallas_call x1, Pallas kernels, attend(): call(kernel, (pltpu.VMEM((devices, 2 * seq_count * heads_dev, head_dim),...  1.82 us
    pallas_call x1, Pallas kernels, body(): call(expert_kernel, (jax.ShapeDtypeStruct((seq_count, model_width), bf16)...  1.32 us
    ppermute x1, waiting for transfers between devices, body(): came = lax.ppermute(send, 'ctx', pairs)  1.07 us
    ppermute x1, waiting for transfers between devices, body(): came = lax.ppermute(mine, 'ctx', pairs)  0.97 us
  transfers between devices with their start and end apart: 2, of which 2 were waited for; matrix products, arithmetic and copies ran while one was open for 0% of the time, Pallas kernels for 0%

profile of v3, /device:TPU:0, one launch (start us, length us, event | category | flops | bytes accessed | tf_op | source)
XLA Modules:
  0.0 40.6 jit_solution(16028088408314850067)
XLA Ops:
  0.0 1.8 %shard_map.109 = (bf16[32,8,128]{2,1,0:T(8,128)(2,1)S(1)}, bf16[256,4096]{1,0:T(8,128)(2,1)S(1)}) custom-call(bf16[128,128]{1,0:T(8,128)(2,1)} %bitcast.15, bf16[2,128,512]{2,1,0:T(8,128)(2,1)} %k_hbm.1, bf16[2,128,512]{2,1,0:T(8,128)(2,1)} %v_hbm.1, bf16[256,4096]{1,0:T(8,128)(2,1)} %w_hbm.1), custom_call_target="tpu_custom_call" | custom-call | flops 1024 | bytes 1024 | tf_op jit(solution)/shard_map/pallas_call | solution.py:109
  1.8 14.5 %all_to_all.15.got_ref = bf16[32,8,128]{2,1,0:T(8,128)(2,1)S(1)} all-to-all(bf16[32,8,128]{2,1,0:T(8,128)(2,1)S(1)} %get-tuple-element.11), channel_id=1, replica_groups=mesh['group'=1,'ctx'=32] {'ctx'}, dimensions={0} | all-to-all | bytes 131072 | tf_op jit(solution)/shard_map/all_to_all | solution.py:235
  16.4 0.6 %shard_map.110 = (f32[2,2048]{1,0:T(2,128)S(1)}, f32[2,2048]{1,0:T(2,128)S(1)}) custom-call(bf16[32,8,128]{2,1,0:T(8,128)(2,1)S(1)} %all_to_all.15.got_ref, bf16[256,4096]{1,0:T(8,128)(2,1)S(1)} %get-tuple-element.12.weight_ref), custom_call_target="tpu_custom_call" | custom-call | flops 1024 | bytes 1024 | tf_op jit(solution)/shard_map/pallas_call | solution.py:261
  17.0 0.2 collective-permute-start
  17.1 1.1 %collective-permute-done.came_ref = f32[2,2048]{1,0:T(2,128)S(1)} collective-permute-done((f32[2,2048]{1,0:T(2,128)S(1)}, f32[2,2048]{1,0:T(2,128)S(1)}, u32[]{:S(2)}, u32[]{:S(2)}) %collective-permute-start) | collective-permute-done | bytes 16416 | tf_op jit(solution)/shard_map/ppermute | solution.py:271
  18.2 0.0 copy-start.4
  18.2 0.0 copy-start
  18.2 0.0 copy-start.1
  18.2 0.0 copy-start.3
  18.2 0.0 copy-start.5
  18.2 0.0 copy-start.6
  18.3 10.2 %all_to_all.16.got_ref = bf16[32,2,1024]{2,1,0:T(2,128)(2,1)S(1)} all-to-all(bf16[32,2,1024]{2,1,0:T(2,128)(2,1)S(1)} %shard_map.111), channel_id=1, replica_groups=mesh['group'=1,'ctx'=32] {'ctx'}, dimensions={0} | all-to-all | bytes 262144 | tf_op jit(solution)/shard_map/all_to_all | solution.py:235
  28.4 0.0 copy-done.4
  28.5 0.3 collective-permute-start.1
  28.8 1.0 %collective-permute-done.1.came_ref = f32[2,2048]{1,0:T(2,128)S(1)} collective-permute-done((f32[2,2048]{1,0:T(2,128)S(1)}, f32[2,2048]{1,0:T(2,128)S(1)}, u32[]{:S(2)}, u32[]{:S(2)}) %collective-permute-start.1) | collective-permute-done | bytes 16416 | tf_op jit(solution)/shard_map/ppermute | solution.py:279
  29.7 0.0 copy-done
  29.7 0.0 copy-done.1
  29.7 0.0 copy-done.2
  29.7 0.0 copy-done.3
  29.7 0.0 copy-done.5
  29.8 0.0 copy-done.6
  29.8 1.3 %shard_map.113 = (bf16[2,4096]{1,0:T(2,128)(2,1)S(1)}, f32[2,128]{1,0:T(2,128)S(1)}) custom-call(f32[2,2048]{1,0:T(2,128)S(1)} %shard_map.112.mine_ref, f32[2,2048]{1,0:T(2,128)S(1)} %collective-permute-done.1.came_ref, f32[1,4096]{1,0:T(1,128)S(1)} %bitcast.13, bf16[192,4096]{1,0:T(8,128)(2,1)S(1)} %bitcast.10, bf16[192,4096]{1,0:T(8,128)(2,1)S(1)} %bitcast.11, ...), custom_call_target="tpu_custom_call" | custom-call | flops 1024 | bytes 1024 | tf_op jit(solution)/shard_map/pallas_call | solution.py:282
  31.1 8.9 %all_to_all.17 = bf16[2,32,128]{2,0,1:T(2,128)(2,1)S(1)} all-to-all(bf16[2,32,128]{2,0,1:T(2,128)(2,1)S(1)} %bitcast.14), channel_id=1, replica_groups=mesh['group'=1,'ctx'=32] {'ctx'}, dimensions={1} | all-to-all | bytes 32768 | tf_op jit(solution)/shard_map/all_to_all | solution.py:300
  40.0 0.6 %add.3 = f32[2,128]{1,0:T(2,128)} add(f32[2,128]{1,0:T(2,128)S(1)} %get-tuple-element.15, f32[2,128]{1,0:T(2,128)S(1)} %convert_reduce_fusion) | non-fusion elementwise | flops 256 | bytes 3072 | tf_op jit(solution)/shard_map/add | solution.py:305
  (4 shorter events, 0.1 us)
Async XLA Ops:
  17.0 1.2 %collective-permute-start = (f32[2,2048]{1,0:T(2,128)S(1)}, f32[2,2048]{1,0:T(2,128)S(1)}, u32[]{:S(2)}, u32[]{:S(2)}) collective-permute-start(f32[2,2048]{1,0:T(2,128)S(1)} %get-tuple-element.14), channel_id=1, source_target_pairs={{0,1},{1,0},{2,3},{3,2},{4,5},{5,4},{6,7},{7,6},{8,9},{9,8},{10,11... | collective-permute-start | bytes 49160 | tf_op jit(solution)/shard_map/ppermute | solution.py:271
  18.2 10.3 %copy-start.4 = (bf16[2,4096]{1,0:T(2,128)(2,1)S(1)}, bf16[2,4096]{1,0:T(2,128)(2,1)}, u32[]{:S(2)}) copy-start(bf16[2,4096]{1,0:T(2,128)(2,1)} %hidden_ref.1) | copy-start | bytes 49156
  18.2 11.5 %copy-start = (bf16[1,4096,192]{1,2,0:T(8,128)(2,1)S(1)}, bf16[1,4096,192]{1,2,0:T(8,128)(2,1)}, u32[]{:S(2)}) copy-start(bf16[1,4096,192]{1,2,0:T(8,128)(2,1)} %param.17) | copy-start | bytes 4718596
  18.2 11.5 %copy-start.1 = (bf16[1,4096,192]{1,2,0:T(8,128)(2,1)S(1)}, bf16[1,4096,192]{1,2,0:T(8,128)(2,1)}, u32[]{:S(2)}) copy-start(bf16[1,4096,192]{1,2,0:T(8,128)(2,1)} %param.18) | copy-start | bytes 4718596
  18.2 11.5 %copy-start.2 = (bf16[1,192,4096]{2,1,0:T(8,128)(2,1)S(1)}, bf16[1,192,4096]{2,1,0:T(8,128)(2,1)}, u32[]{:S(2)}) copy-start(bf16[1,192,4096]{2,1,0:T(8,128)(2,1)} %param.19) | copy-start | bytes 4718596
  18.2 11.5 %copy-start.3 = (f32[4096]{0:T(1024)S(1)}, f32[4096]{0:T(1024)}, u32[]{:S(2)}) copy-start(f32[4096]{0:T(1024)} %param.16) | copy-start | bytes 49156
  18.2 11.5 %copy-start.5 = (s32[2,4]{1,0:T(2,128)S(1)}, s32[2,4]{1,0:T(2,128)}, u32[]{:S(2)}) copy-start(s32[2,4]{1,0:T(2,128)} %routes_ref.1) | copy-start | bytes 100
  18.2 11.5 %copy-start.6 = (f32[2,4]{1,0:T(2,128)S(1)}, f32[2,4]{1,0:T(2,128)}, u32[]{:S(2)}) copy-start(f32[2,4]{1,0:T(2,128)} %share_ref.1) | copy-start | bytes 100
  28.5 1.2 %collective-permute-start.1 = (f32[2,2048]{1,0:T(2,128)S(1)}, f32[2,2048]{1,0:T(2,128)S(1)}, u32[]{:S(2)}, u32[]{:S(2)}) collective-permute-start(f32[2,2048]{1,0:T(2,128)S(1)} %shard_map.112.mine_ref), channel_id=1, source_target_pairs={{0,1},{1,0},{2,3},{3,2},{4,5},{5,4},{6,7},{7,6},{8,9},{9,8},{10,11... | collective-permute-start | bytes 49160 | tf_op jit(solution)/shard_map/ppermute | solution.py:279

commit v4 on v3

--- a/solution.py
+++ b/solution.py
@@ -43,11 +43,11 @@
     return lax.dot_general(a, b, (((1,), (1,)), ((), ())), preferred_element_type=f32)
 
 
-def attend_kernel(heads_dev, kv_heads, q_hbm, k_hbm, v_hbm, w_hbm, out_ref, w_ref, q, k, v, sems):
+def attend_kernel(heads_dev, kv_heads, q_hbm, k_hbm, v_hbm, out_ref, q, k, v, sems):
     seq_count, local_len, _ = k.shape
     head_dim = q.shape[1]
     head_count = q.shape[0] // seq_count
-    moves = ((q_hbm, q), (k_hbm, k), (v_hbm, v), (w_hbm, w_ref))
+    moves = ((k_hbm, k), (q_hbm, q), (v_hbm, v))
     copies = [pltpu.make_async_copy(src, dst, sems.at[n]) for n, (src, dst) in enumerate(moves)]
     for copy in copies:
         copy.start()
@@ -73,9 +73,10 @@
             [jnp.where(seq_of == s, values, 0.0).astype(bf16) for s in range(seq_count)], axis=1
         )
 
+    copies[1].wait()
+    queries = [by_seq(jnp.dot(pick, q[...], preferred_element_type=f32)) for pick in picks]
     copies[0].wait()
-    queries = [by_seq(jnp.dot(pick, q[...], preferred_element_type=f32)) for pick in picks]
-    copies[1].wait()
+    copies[2].wait()
     feats = [slice(g * head_dim, (g + 1) * head_dim) for g in range(kv_heads)]
     scores = [
         dot_nt(queries[g], jnp.concatenate([k[s, :, feats[g]] for s in range(seq_count)], axis=1))
@@ -92,57 +93,60 @@
         totals = jnp.where(lane < 2 * third, coarse, denom - coarse)
         stats.append(jnp.where(lane < third, peak, totals))
         numers.append(by_seq(numer))
-    copies[2].wait()
     for g in range(kv_heads):
         values = jnp.concatenate([v[s, :, feats[g]] for s in range(seq_count)], axis=0)
         part = jnp.dot(numers[g], values, preferred_element_type=f32)
         block = jnp.where(is_part, part, stats[g]).astype(bf16)
         out_ref[g * owners : (g + 1) * owners] = block.reshape(owners, 2 * half, head_dim)
-    copies[3].wait()
-
-
-def attend(queries, key_cache, value_cache, out_weight, devices, heads_dev):
+
+
+def attend(queries, key_cache, value_cache, devices, heads_dev):
     seq_count, head_count, head_dim = queries.shape
     hbm = pl.BlockSpec(memory_space=pltpu.HBM)
     q = queries.reshape(seq_count * head_count, head_dim)
     kernel = functools.partial(attend_kernel, heads_dev, key_cache.shape[2] // head_dim)
     return call(
         kernel,
-        (
-            pltpu.VMEM((devices, 2 * seq_count * heads_dev, head_dim), bf16),
-            pltpu.VMEM(out_weight.shape, bf16),
-        ),
-        in_specs=[hbm] * 4,
+        pltpu.VMEM((devices, 2 * seq_count * heads_dev, head_dim), bf16),
+        in_specs=[hbm] * 3,
         scratch=(
             pltpu.VMEM(q.shape, bf16),
             pltpu.VMEM(key_cache.shape, bf16),
             pltpu.VMEM(value_cache.shape, bf16),
-            pltpu.SemaphoreType.DMA((4,)),
+            pltpu.SemaphoreType.DMA((3,)),
         ),
-    )(in_hbm(q), in_hbm(key_cache), in_hbm(value_cache), in_hbm(out_weight))
-
-
-def project_kernel(seq_count, got_ref, weight_ref, send_ref, keep_ref):
+        flops=LONG,
+    )(in_hbm(q), in_hbm(key_cache), in_hbm(value_cache))
+
+
+def columns(block, width):
+    return pl.ds(pl.multiple_of(block * width, width), width)
+
+
+def send_kernel(seq_count, got_ref, weight_ref, send_ref, attended_ref):
     core = lax.rem(lax.axis_index("ctx"), 2)
     head_dim = got_ref.shape[2]
     half = got_ref.shape[1] // 2
     got = got_ref[...].astype(f32)
     third = head_dim // 3
     stats = got[:, half:, :]
-    peaks = stats[:, :, 0:1]
-    scale = jnp.exp(peaks - jnp.max(peaks, axis=0, keepdims=True))
-    total = stats[:, :, third : third + 1] + stats[:, :, 2 * third : 2 * third + 1]
-    denoms = jnp.sum(scale * total, axis=0)
+    scale = jnp.exp(stats - jnp.max(stats, axis=0, keepdims=True))[:, :, 0:1]
+    totals = jnp.sum(scale * stats, axis=0)
+    denoms = totals[:, third : third + 1] + totals[:, 2 * third : 2 * third + 1]
     summed = jnp.sum(scale * got[:, :half, :], axis=0)
     attended = (summed / denoms).astype(bf16)
     attended = jnp.concatenate(
         [attended[n : n + seq_count] for n in range(0, half, seq_count)], axis=1
     )
-    mid = weight_ref.shape[1] // 2
-    low = jnp.dot(attended, weight_ref[:, :mid], preferred_element_type=f32)
-    high = jnp.dot(attended, weight_ref[:, mid:], preferred_element_type=f32)
-    send_ref[...] = jnp.where(core == 0, high, low)
-    keep_ref[...] = jnp.where(core == 0, low, high)
+    attended_ref[...] = attended
+    other = columns(1 - core, send_ref.shape[1])
+    send_ref[...] = jnp.dot(attended, weight_ref[:, other], preferred_element_type=f32)
+
+
+def keep_kernel(attended_ref, weight_ref, keep_ref):
+    core = lax.rem(lax.axis_index("ctx"), 2)
+    own = columns(core, keep_ref.shape[1])
+    keep_ref[...] = jnp.dot(attended_ref[...], weight_ref[:, own], preferred_element_type=f32)
 
 
 def spread_kernel(keep_ref, came_ref, out_ref):
@@ -168,32 +172,63 @@
         out_ref[:, side * quarter : (side + 1) * quarter] = hidden + total
 
 
+def gated(core, half_ref, gain_ref, weight_refs):
+    quarter = half_ref.shape[1] // 2
+    acts = [None] * len(weight_refs)
+    for side in range(2):
+        cols = columns(2 * side + core, quarter)
+        rows = half_ref[:, side * quarter : (side + 1) * quarter]
+        rows = (rows * gain_ref[:, cols]).astype(bf16)
+        for n, weight_ref in enumerate(weight_refs):
+            act = dot_nt(rows, weight_ref[:, cols])
+            acts[n] = act if side == 0 else acts[n] + act
+    return acts
+
+
+def squares(half_ref):
+    return jnp.sum(half_ref[...] * half_ref[...], axis=1, keepdims=True)
+
+
+def own_half_kernel(mine_ref, gain_ref, gate_ref, up_ref, down_ref, gate_out, up_out):
+    del down_ref
+    core = lax.rem(lax.axis_index("ctx"), 2)
+    gate_out[...], up_out[...] = gated(core, mine_ref, gain_ref, (gate_ref, up_ref))
+
+
 def expert_kernel(
-    mine_ref, came_ref, gain_ref, gate_ref, up_ref, down_ref, routes_ref, share_ref, out_ref, mine_out, resid_ref
+    mine_ref,
+    came_ref,
+    gate_part,
+    up_part,
+    gain_ref,
+    gate_ref,
+    up_ref,
+    down_ref,
+    routes_ref,
+    share_ref,
+    out_ref,
+    mine_out,
+    resid_ref,
 ):
     index = lax.axis_index("ctx")
     core = lax.rem(index, 2)
     expert = lax.div(index, QUARTERS)
-    mid = mine_ref.shape[1]
-    even = jnp.where(core == 0, mine_ref[...], came_ref[...])
-    odd = jnp.where(core == 0, came_ref[...], mine_ref[...])
-    low = jnp.concatenate([even[:, : mid // 2], odd[:, : mid // 2]], axis=1)
-    high = jnp.concatenate([even[:, mid // 2 :], odd[:, mid // 2 :]], axis=1)
-    resid_ref[:, :mid] = low
-    resid_ref[:, mid:] = high
+    quarter = mine_ref.shape[1] // 2
+    gate_act, up_act = gated(1 - core, came_ref, gain_ref, (gate_ref, up_ref))
+    square = squares(mine_ref) + squares(came_ref)
+    inverse_rms = lax.rsqrt(square / (4 * quarter) + eps)
+    gate_act = (gate_act + gate_part[...]) * inverse_rms
+    up_act = (up_act + up_part[...]) * inverse_rms
+    hidden = (gate_act / (1.0 + jnp.exp(-gate_act)) * up_act).astype(bf16)
+    for side in range(2):
+        cut = slice(side * quarter, (side + 1) * quarter)
+        resid_ref[:, columns(2 * side + core, quarter)] = mine_ref[:, cut]
+        resid_ref[:, columns(2 * side + 1 - core, quarter)] = came_ref[:, cut]
     col_dev = mine_out.shape[1]
-    if col_dev == 2 * mid:
+    if col_dev == resid_ref.shape[1]:
         mine_out[...] = resid_ref[...]
     else:
-        start = pl.multiple_of(index * col_dev, col_dev)
-        mine_out[...] = resid_ref[:, pl.ds(start, col_dev)]
-    square = jnp.sum(low * low, axis=1, keepdims=True) + jnp.sum(high * high, axis=1, keepdims=True)
-    inverse_rms = lax.rsqrt(square / (2 * mid) + eps)
-    low = (low * inverse_rms * gain_ref[:, :mid]).astype(bf16)
-    high = (high * inverse_rms * gain_ref[:, mid:]).astype(bf16)
-    gate_act = dot_nt(low, gate_ref[:, :mid]) + dot_nt(high, gate_ref[:, mid:])
-    up_act = dot_nt(low, up_ref[:, :mid]) + dot_nt(high, up_ref[:, mid:])
-    hidden = (gate_act / (1.0 + jnp.exp(-gate_act)) * up_act).astype(bf16)
+        mine_out[...] = resid_ref[:, columns(index, col_dev)]
     share = jnp.where(routes_ref[...] == expert, share_ref[...], 0.0)
     share = jnp.sum(share, axis=1, keepdims=True)
     out = jnp.dot(hidden, down_ref[...], preferred_element_type=f32)
@@ -257,10 +292,15 @@
     half = jax.ShapeDtypeStruct((seq_count, mid), f32)
     if feat_dev % head_dim == 0:
         heads_dev = feat_dev // head_dim
-        parts, weight = attend(queries, key_cache, value_cache, out_weight, devices, heads_dev)
-        send, keep = call(functools.partial(project_kernel, seq_count), (half, half), count=2)(
-            swap_blocks(parts), weight
-        )
+        parts = attend(queries, key_cache, value_cache, devices, heads_dev)
+        got = swap_blocks(parts)
+        weight = in_vmem(out_weight)
+        send, attended = call(
+            functools.partial(send_kernel, seq_count),
+            (half, jax.ShapeDtypeStruct((seq_count, feat_dev), bf16)),
+            count=2,
+        )(got, weight)
+        keep = call(keep_kernel, half, count=2)(attended, weight)
     else:
         attended = merge_parts(queries, key_cache, value_cache, devices)
         proj = jnp.dot(attended, out_weight, preferred_element_type=f32)
@@ -279,21 +319,30 @@
     came = lax.ppermute(mine, "ctx", pairs)
     col_dev = model_width // devices
     aligned = col_dev % 128 == 0
+    gain = norm_gain.reshape(1, model_width)
+    gate, up = in_vmem(gate_weight[0].T), in_vmem(up_weight[0].T)
+    down = in_vmem(down_weight[0])
+    act = jax.ShapeDtypeStruct((seq_count, gate.shape[0]), f32)
+    gate_part, up_part = call(own_half_kernel, (act, act), count=5)(
+        mine, gain, gate, up, down
+    )
     out, resid_mine = call(
         expert_kernel,
         (
             jax.ShapeDtypeStruct((seq_count, model_width), bf16),
             jax.ShapeDtypeStruct((seq_count, col_dev if aligned else model_width), f32),
         ),
-        count=8,
+        count=10,
         scratch=(pltpu.VMEM((seq_count, model_width), f32),),
     )(
         mine,
         came,
-        norm_gain.reshape(1, model_width),
-        in_vmem(gate_weight[0].T),
-        in_vmem(up_weight[0].T),
-        in_vmem(down_weight[0]),
+        gate_part,
+        up_part,
+        gain,
+        gate,
+        up,
+        down,
         routes,
         route_weight,
     )

time: 40.8 us -> 39.7 us (0.973)
  waiting for transfers between devices: 2.04 us -> 1.19 us
    ppermute x1, waiting for transfers between devices: 0.97 us -> 0.41 us  [body(): came = lax.ppermute(mine, 'ctx', pairs)]
    pallas_call x1, Pallas kernels: 1.32 us -> 0.83 us  [body(): call(expert_kernel, (jax.ShapeDtypeStruct((seq_count, model_width), bf16)...]
    pallas_call x2 -> x4, Pallas kernels: 2.42 us -> 2.89 us  [the longest x1 1.64 us: attend(): call(kernel, pltpu.VMEM((devices, 2 * seq_count * heads_dev, head_dim), b...]
  transfers between devices with their start and end apart: 2 -> 2, of which waited for: 2 -> 2; matrix products, arithmetic and copies ran while one was open for 0% -> 0% of each run, Pallas kernels for 0% -> 2%
where the time goes in v4:
time: 39.7 us; the launch traced here: 39.6 us
  blocking collectives  33.4 us (84%)
  Pallas kernels  3.76 us (9%)
  waiting for transfers between devices  1.19 us (3%)
  other arithmetic  0.61 us (2%)
  starting transfers between devices  0.43 us (1%)
    all_to_all x2, blocking collectives, swap_blocks(): lax.all_to_all(blocks, 'ctx', split_axis=0, concat_axis=0, tiled=True)  24.6 us
    all_to_all x1, blocking collectives, body(): lax.all_to_all(out.reshape(seq_count, devices, col_dev), 'ctx', split_axi...  8.86 us
    pallas_call x1, Pallas kernels, attend(): call(kernel, pltpu.VMEM((devices, 2 * seq_count * heads_dev, head_dim), b...  1.64 us
    pallas_call x1, Pallas kernels, body(): call(expert_kernel, (jax.ShapeDtypeStruct((seq_count, model_width), bf16)...  0.83 us
  transfers between devices with their start and end apart: 2, of which 2 were waited for; matrix products, arithmetic and copies ran while one was open for 0% of the time, Pallas kernels for 2%

profile of v4, /device:TPU:0, one launch (start us, length us, event | category | flops | bytes accessed | tf_op | source)
XLA Modules:
  0.0 39.6 jit_solution(11248521226481844341)
XLA Ops:
  0.0 1.6 %shard_map.109 = bf16[32,8,128]{2,1,0:T(8,128)(2,1)S(1)} custom-call(bf16[128,128]{1,0:T(8,128)(2,1)} %bitcast.19, bf16[2,128,512]{2,1,0:T(8,128)(2,1)} %k_hbm.1, bf16[2,128,512]{2,1,0:T(8,128)(2,1)} %v_hbm.1), custom_call_target="tpu_custom_call" | custom-call | flops 17179869184 | bytes 1024 | tf_op jit(solution)/shard_map/pallas_call | solution.py:108
  1.7 14.5 %all_to_all.15.got_ref = bf16[32,8,128]{2,1,0:T(8,128)(2,1)S(1)} all-to-all(bf16[32,8,128]{2,1,0:T(8,128)(2,1)S(1)} %shard_map.109), channel_id=1, replica_groups=mesh['group'=1,'ctx'=32] {'ctx'}, dimensions={0} | all-to-all | bytes 131072 | tf_op jit(solution)/shard_map/all_to_all | solution.py:270
  16.2 0.0 copy-done
  16.2 0.5 %shard_map.110 = (f32[2,2048]{1,0:T(2,128)S(1)}, bf16[2,256]{1,0:T(2,128)(2,1)S(1)}) custom-call(bf16[32,8,128]{2,1,0:T(8,128)(2,1)S(1)} %all_to_all.15.got_ref, bf16[256,4096]{1,0:T(8,128)(2,1)S(1)} %copy-done), custom_call_target="tpu_custom_call" | custom-call | flops 1024 | bytes 1024 | tf_op jit(solution)/shard_map/pallas_call | solution.py:298
  16.7 0.1 collective-permute-start
  16.8 0.2 shard_map.111.keep_ref
  17.1 0.0 copy-start.2
  17.1 0.0 copy-start.3
  17.1 0.0 copy-start.4
  17.1 0.8 %collective-permute-done.came_ref = f32[2,2048]{1,0:T(2,128)S(1)} collective-permute-done((f32[2,2048]{1,0:T(2,128)S(1)}, f32[2,2048]{1,0:T(2,128)S(1)}, u32[]{:S(2)}, u32[]{:S(2)}) %collective-permute-start) | collective-permute-done | bytes 16416 | tf_op jit(solution)/shard_map/ppermute | solution.py:311
  17.9 10.0 %all_to_all.16.got_ref = bf16[32,2,1024]{2,1,0:T(2,128)(2,1)S(1)} all-to-all(bf16[32,2,1024]{2,1,0:T(2,128)(2,1)S(1)} %shard_map.112), channel_id=1, replica_groups=mesh['group'=1,'ctx'=32] {'ctx'}, dimensions={0} | all-to-all | bytes 262144 | tf_op jit(solution)/shard_map/all_to_all | solution.py:270
  28.0 0.0 copy-done.5
  28.0 0.3 collective-permute-start.1
  28.3 0.0 copy-done.1
  28.3 0.0 copy-done.2
  28.3 0.0 copy-done.4
  28.3 0.0 copy-start.6
  28.3 0.0 copy-start.7
  28.3 0.5 %shard_map.114 = (f32[2,192]{1,0:T(2,128)S(1)}, f32[2,192]{1,0:T(2,128)S(1)}) custom-call(f32[2,2048]{1,0:T(2,128)S(1)} %shard_map.113.mine_ref, f32[1,4096]{1,0:T(1,128)S(1)} %bitcast.16, bf16[192,4096]{1,0:T(8,128)(2,1)S(1)} %bitcast.10, bf16[192,4096]{1,0:T(8,128)(2,1)S(1)} %bitcast.12, bf16[192,4096]{1,0:T(8,128)(2,1)S(1)} %bitcast.14), custom_call_target="tpu_custom_call" | custom-call | flops 1024 | bytes 1024 | tf_op jit(solution)/shard_map/pallas_call | solution.py:326
  28.8 0.4 %collective-permute-done.1.came_ref = f32[2,2048]{1,0:T(2,128)S(1)} collective-permute-done((f32[2,2048]{1,0:T(2,128)S(1)}, f32[2,2048]{1,0:T(2,128)S(1)}, u32[]{:S(2)}, u32[]{:S(2)}) %collective-permute-start.1) | collective-permute-done | bytes 16416 | tf_op jit(solution)/shard_map/ppermute | solution.py:319
  29.2 0.0 copy-done.7
  29.2 0.8 %shard_map.115 = (bf16[2,4096]{1,0:T(2,128)(2,1)S(1)}, f32[2,128]{1,0:T(2,128)S(1)}) custom-call(f32[2,2048]{1,0:T(2,128)S(1)} %shard_map.113.mine_ref, f32[2,2048]{1,0:T(2,128)S(1)} %collective-permute-done.1.came_ref, f32[2,192]{1,0:T(2,128)S(1)} %get-tuple-element.13.gate_part, f32[2,192]{1,0:T(2,128)S(1)} %get-tuple-element.14.up_part, ...), custom_call_target="tpu_custom_call" | custom-call | flops 1024 | bytes 1024 | tf_op jit(solution)/shard_map/pallas_call | solution.py:329
  30.1 8.9 %all_to_all.17 = bf16[2,32,128]{2,0,1:T(2,128)(2,1)S(1)} all-to-all(bf16[2,32,128]{2,0,1:T(2,128)(2,1)S(1)} %bitcast.18), channel_id=1, replica_groups=mesh['group'=1,'ctx'=32] {'ctx'}, dimensions={1} | all-to-all | bytes 32768 | tf_op jit(solution)/shard_map/all_to_all | solution.py:349
  39.0 0.6 %add.3 = f32[2,128]{1,0:T(2,128)} add(f32[2,128]{1,0:T(2,128)S(1)} %get-tuple-element.15, f32[2,128]{1,0:T(2,128)S(1)} %convert_reduce_fusion) | non-fusion elementwise | flops 256 | bytes 3072 | tf_op jit(solution)/shard_map/add | solution.py:354
  (8 shorter events, 0.1 us)
Async XLA Ops:
  0.0 16.2 %copy-start = (bf16[256,4096]{1,0:T(8,128)(2,1)S(1)}, bf16[256,4096]{1,0:T(8,128)(2,1)}, u32[]{:S(2)}) copy-start(bf16[256,4096]{1,0:T(8,128)(2,1)} %weight_ref.3) | copy-start | bytes 6291460
  16.7 1.2 %collective-permute-start = (f32[2,2048]{1,0:T(2,128)S(1)}, f32[2,2048]{1,0:T(2,128)S(1)}, u32[]{:S(2)}, u32[]{:S(2)}) collective-permute-start(f32[2,2048]{1,0:T(2,128)S(1)} %get-tuple-element.12), channel_id=1, source_target_pairs={{0,1},{1,0},{2,3},{3,2},{4,5},{5,4},{6,7},{7,6},{8,9},{9,8},{10,11... | collective-permute-start | bytes 49160 | tf_op jit(solution)/shard_map/ppermute | solution.py:311
  17.1 10.9 %copy-start.5 = (bf16[2,4096]{1,0:T(2,128)(2,1)S(1)}, bf16[2,4096]{1,0:T(2,128)(2,1)}, u32[]{:S(2)}) copy-start(bf16[2,4096]{1,0:T(2,128)(2,1)} %hidden_ref.1) | copy-start | bytes 49156
  17.1 11.2 %copy-start.1 = (bf16[1,4096,192]{1,2,0:T(8,128)(2,1)S(1)}, bf16[1,4096,192]{1,2,0:T(8,128)(2,1)}, u32[]{:S(2)}) copy-start(bf16[1,4096,192]{1,2,0:T(8,128)(2,1)} %param.17) | copy-start | bytes 4718596
  17.1 11.2 %copy-start.2 = (bf16[1,4096,192]{1,2,0:T(8,128)(2,1)S(1)}, bf16[1,4096,192]{1,2,0:T(8,128)(2,1)}, u32[]{:S(2)}) copy-start(bf16[1,4096,192]{1,2,0:T(8,128)(2,1)} %param.18) | copy-start | bytes 4718596
  17.1 11.2 %copy-start.3 = (bf16[1,192,4096]{2,1,0:T(8,128)(2,1)S(1)}, bf16[1,192,4096]{2,1,0:T(8,128)(2,1)}, u32[]{:S(2)}) copy-start(bf16[1,192,4096]{2,1,0:T(8,128)(2,1)} %param.19) | copy-start | bytes 4718596
  17.1 11.2 %copy-start.4 = (f32[4096]{0:T(1024)S(1)}, f32[4096]{0:T(1024)}, u32[]{:S(2)}) copy-start(f32[4096]{0:T(1024)} %param.16) | copy-start | bytes 49156
  28.0 1.2 %collective-permute-start.1 = (f32[2,2048]{1,0:T(2,128)S(1)}, f32[2,2048]{1,0:T(2,128)S(1)}, u32[]{:S(2)}, u32[]{:S(2)}) collective-permute-start(f32[2,2048]{1,0:T(2,128)S(1)} %shard_map.113.mine_ref), channel_id=1, source_target_pairs={{0,1},{1,0},{2,3},{3,2},{4,5},{5,4},{6,7},{7,6},{8,9},{9,8},{10,11... | collective-permute-start | bytes 49160 | tf_op jit(solution)/shard_map/ppermute | solution.py:319
  28.3 1.0 %copy-start.6 = (s32[2,4]{1,0:T(2,128)S(1)}, s32[2,4]{1,0:T(2,128)}, u32[]{:S(2)}) copy-start(s32[2,4]{1,0:T(2,128)} %routes_ref.1) | copy-start | bytes 100
  28.3 0.9 %copy-start.7 = (f32[2,4]{1,0:T(2,128)S(1)}, f32[2,4]{1,0:T(2,128)}, u32[]{:S(2)}) copy-start(f32[2,4]{1,0:T(2,128)} %share_ref.1) | copy-start | bytes 100

commit v5 on v4

--- a/solution.py
+++ b/solution.py
@@ -43,28 +43,34 @@
     return lax.dot_general(a, b, (((1,), (1,)), ((), ())), preferred_element_type=f32)
 
 
-def attend_kernel(heads_dev, kv_heads, q_hbm, k_hbm, v_hbm, out_ref, q, k, v, sems):
+def rows_of(heads_dev, seq_count, owners):
+    half = seq_count * heads_dev
+    row = lax.broadcasted_iota(jnp.int32, (owners * 2 * half, 1), 0)
+    within = lax.rem(row, half)
+    seq_of = lax.rem(within, seq_count)
+    head_of = lax.div(row, 2 * half) * heads_dev + lax.div(within, seq_count)
+    return seq_of, head_of, lax.rem(row, 2 * half) < half
+
+
+def score_kernel(
+    heads_dev, kv_heads, q_hbm, k_hbm, v_hbm, numer_ref, stat_ref, v_ref, q, k, sems
+):
     seq_count, local_len, _ = k.shape
     head_dim = q.shape[1]
     head_count = q.shape[0] // seq_count
-    moves = ((k_hbm, k), (q_hbm, q), (v_hbm, v))
+    moves = ((k_hbm, k), (q_hbm, q), (v_hbm, v_ref))
     copies = [pltpu.make_async_copy(src, dst, sems.at[n]) for n, (src, dst) in enumerate(moves)]
     for copy in copies:
         copy.start()
-    half = seq_count * heads_dev
     owners = head_count // kv_heads // heads_dev
-    rows = owners * 2 * half
-    row = lax.broadcasted_iota(jnp.int32, (rows, 1), 0)
-    within = lax.rem(row, half)
-    seq_of = lax.rem(within, seq_count)
-    head_of = lax.div(row, 2 * half) * heads_dev + lax.div(within, seq_count)
+    seq_of, head_of, _ = rows_of(heads_dev, seq_count, owners)
+    rows = seq_of.shape[0]
     source = seq_of * head_count + head_of
     column = lax.broadcasted_iota(jnp.int32, (rows, q.shape[0]), 1)
     picks = [
         jnp.where(column == source + g * owners * heads_dev, 1.0, 0.0).astype(bf16)
         for g in range(kv_heads)
     ]
-    is_part = lax.rem(row, 2 * half) < half
     lane = lax.broadcasted_iota(jnp.int32, (rows, head_dim), 1)
     third = head_dim // 3
 
@@ -77,46 +83,60 @@
     queries = [by_seq(jnp.dot(pick, q[...], preferred_element_type=f32)) for pick in picks]
     copies[0].wait()
     copies[2].wait()
-    feats = [slice(g * head_dim, (g + 1) * head_dim) for g in range(kv_heads)]
-    scores = [
-        dot_nt(queries[g], jnp.concatenate([k[s, :, feats[g]] for s in range(seq_count)], axis=1))
-        * head_dim ** (-0.5)
-        for g in range(kv_heads)
-    ]
-    numers = []
-    stats = []
     for g in range(kv_heads):
-        peak = jnp.max(scores[g], axis=1, keepdims=True).astype(bf16).astype(f32)
-        numer = jnp.exp(scores[g] - peak)
+        cut = slice(g * head_dim, (g + 1) * head_dim)
+        keys = jnp.concatenate([k[s, :, cut] for s in range(seq_count)], axis=1)
+        scores = dot_nt(queries[g], keys) * head_dim ** (-0.5)
+        peak = jnp.max(scores, axis=1, keepdims=True).astype(bf16).astype(f32)
+        numer = jnp.exp(scores - peak)
         denom = jnp.sum(numer, axis=1, keepdims=True)
         coarse = denom.astype(bf16).astype(f32)
         totals = jnp.where(lane < 2 * third, coarse, denom - coarse)
-        stats.append(jnp.where(lane < third, peak, totals))
-        numers.append(by_seq(numer))
+        stat_ref[g * rows : (g + 1) * rows] = jnp.where(lane < third, peak, totals)
+        numer_ref[g * rows : (g + 1) * rows] = by_seq(numer)
+
+
+def value_kernel(heads_dev, kv_heads, numer_ref, stat_ref, v_ref, out_ref):
+    seq_count = v_ref.shape[0]
+    head_dim = stat_ref.shape[1]
+    owners = out_ref.shape[0] // kv_heads
+    _, _, is_part = rows_of(heads_dev, seq_count, owners)
+    rows = is_part.shape[0]
     for g in range(kv_heads):
-        values = jnp.concatenate([v[s, :, feats[g]] for s in range(seq_count)], axis=0)
-        part = jnp.dot(numers[g], values, preferred_element_type=f32)
-        block = jnp.where(is_part, part, stats[g]).astype(bf16)
-        out_ref[g * owners : (g + 1) * owners] = block.reshape(owners, 2 * half, head_dim)
+        cut = slice(g * head_dim, (g + 1) * head_dim)
+        own = slice(g * rows, (g + 1) * rows)
+        values = jnp.concatenate([v_ref[s, :, cut] for s in range(seq_count)], axis=0)
+        part = jnp.dot(numer_ref[own], values, preferred_element_type=f32)
+        block = jnp.where(is_part, part, stat_ref[own]).astype(bf16)
+        out_ref[g * owners : (g + 1) * owners] = block.reshape(owners, -1, head_dim)
 
 
 def attend(queries, key_cache, value_cache, devices, heads_dev):
     seq_count, head_count, head_dim = queries.shape
+    kv_heads = key_cache.shape[2] // head_dim
     hbm = pl.BlockSpec(memory_space=pltpu.HBM)
     q = queries.reshape(seq_count * head_count, head_dim)
-    kernel = functools.partial(attend_kernel, heads_dev, key_cache.shape[2] // head_dim)
-    return call(
-        kernel,
-        pltpu.VMEM((devices, 2 * seq_count * heads_dev, head_dim), bf16),
+    rows = 2 * q.shape[0]
+    numers, stats, values = call(
+        functools.partial(score_kernel, heads_dev, kv_heads),
+        (
+            pltpu.VMEM((rows, seq_count * key_cache.shape[1]), bf16),
+            pltpu.VMEM((rows, head_dim), f32),
+            pltpu.VMEM(value_cache.shape, bf16),
+        ),
         in_specs=[hbm] * 3,
         scratch=(
             pltpu.VMEM(q.shape, bf16),
             pltpu.VMEM(key_cache.shape, bf16),
-            pltpu.VMEM(value_cache.shape, bf16),
             pltpu.SemaphoreType.DMA((3,)),
         ),
+    )(in_hbm(q), in_hbm(key_cache), in_hbm(value_cache))
+    return call(
+        functools.partial(value_kernel, heads_dev, kv_heads),
+        pltpu.VMEM((devices, 2 * seq_count * heads_dev, head_dim), bf16),
+        count=3,
         flops=LONG,
-    )(in_hbm(q), in_hbm(key_cache), in_hbm(value_cache))
+    )(numers, stats, values)
 
 
 def columns(block, width):
@@ -313,7 +333,6 @@
         spread_kernel,
         jax.ShapeDtypeStruct((devices, seq_count, mid // 2), bf16),
         count=2,
-        flops=LONG,
     )(keep, came)
     mine = call(resid_kernel, half, count=2)(swap_blocks(spread), hidden_in)
     came = lax.ppermute(mine, "ctx", pairs)

time: 39.7 us -> 39.7 us (level)
    pallas_call x1 -> x2, Pallas kernels: 1.64 us -> 1.62 us  [the longest x1 1.45 us: attend(): call(functools.partial(score_kernel, heads_dev, kv_heads), (pltpu.VMEM((r...]
where the time goes in v5:
time: 39.7 us; the launch traced here: 39.5 us
  blocking collectives  33.3 us (84%)
  Pallas kernels  3.75 us (9%)
  waiting for transfers between devices  1.24 us (3%)
  other arithmetic  0.61 us (2%)
  starting transfers between devices  0.46 us (1%)
    all_to_all x2, blocking collectives, swap_blocks(): lax.all_to_all(blocks, 'ctx', split_axis=0, concat_axis=0, tiled=True)  24.5 us
    all_to_all x1, blocking collectives, body(): lax.all_to_all(out.reshape(seq_count, devices, col_dev), 'ctx', split_axi...  8.86 us
    pallas_call x1, Pallas kernels, attend(): call(functools.partial(score_kernel, heads_dev, kv_heads), (pltpu.VMEM((r...  1.45 us
    pallas_call x1, Pallas kernels, body(): call(expert_kernel, (jax.ShapeDtypeStruct((seq_count, model_width), bf16)...  0.83 us
    ppermute x1, waiting for transfers between devices, body(): came = lax.ppermute(send, 'ctx', pairs)  0.83 us
  transfers between devices with their start and end apart: 2, of which 2 were waited for; matrix products, arithmetic and copies ran while one was open for 0% of the time, Pallas kernels for 2%

profile of v5, /device:TPU:0, one launch (start us, length us, event | category | flops | bytes accessed | tf_op | source)
XLA Modules:
  0.0 39.5 jit_solution(10376769079349963257)
XLA Ops:
  0.0 1.4 %shard_map.109 = (bf16[256,256]{1,0:T(8,128)(2,1)S(1)}, f32[256,128]{1,0:T(8,128)S(1)}, bf16[2,128,512]{2,1,0:T(8,128)(2,1)S(1)}) custom-call(bf16[128,128]{1,0:T(8,128)(2,1)} %bitcast.19, bf16[2,128,512]{2,1,0:T(8,128)(2,1)} %k_hbm.1, bf16[2,128,512]{2,1,0:T(8,128)(2,1)} %v_hbm.1), custom_call_target="tpu_custom_call" | custom-call | flops 1024 | bytes 1024 | tf_op jit(solution)/shard_map/pallas_call | solution.py:120
  1.5 0.0 copy-start
  1.5 0.2 shard_map.110
  1.6 14.5 %all_to_all.15.got_ref = bf16[32,8,128]{2,1,0:T(8,128)(2,1)S(1)} all-to-all(bf16[32,8,128]{2,1,0:T(8,128)(2,1)S(1)} %shard_map.110), channel_id=1, replica_groups=mesh['group'=1,'ctx'=32] {'ctx'}, dimensions={0} | all-to-all | bytes 131072 | tf_op jit(solution)/shard_map/all_to_all | solution.py:290
  16.2 0.0 copy-done
  16.2 0.5 %shard_map.111 = (f32[2,2048]{1,0:T(2,128)S(1)}, bf16[2,256]{1,0:T(2,128)(2,1)S(1)}) custom-call(bf16[32,8,128]{2,1,0:T(8,128)(2,1)S(1)} %all_to_all.15.got_ref, bf16[256,4096]{1,0:T(8,128)(2,1)S(1)} %copy-done), custom_call_target="tpu_custom_call" | custom-call | flops 1024 | bytes 1024 | tf_op jit(solution)/shard_map/pallas_call | solution.py:318
  16.7 0.2 collective-permute-start
  16.9 0.2 shard_map.112.keep_ref
  17.1 0.8 %collective-permute-done.came_ref = f32[2,2048]{1,0:T(2,128)S(1)} collective-permute-done((f32[2,2048]{1,0:T(2,128)S(1)}, f32[2,2048]{1,0:T(2,128)S(1)}, u32[]{:S(2)}, u32[]{:S(2)}) %collective-permute-start) | collective-permute-done | bytes 16416 | tf_op jit(solution)/shard_map/ppermute | solution.py:331
  18.0 9.9 %all_to_all.16.got_ref = bf16[32,2,1024]{2,1,0:T(2,128)(2,1)S(1)} all-to-all(bf16[32,2,1024]{2,1,0:T(2,128)(2,1)S(1)} %shard_map.113), channel_id=1, replica_groups=mesh['group'=1,'ctx'=32] {'ctx'}, dimensions={0} | all-to-all | bytes 262144 | tf_op jit(solution)/shard_map/all_to_all | solution.py:290
  27.9 0.0 copy-done.5
  27.9 0.3 collective-permute-start.1
  28.2 0.0 copy-done.2
  28.2 0.0 copy-done.3
  28.2 0.0 copy-done.1
  28.2 0.0 copy-done.4
  28.2 0.0 copy-start.6
  28.2 0.0 copy-start.7
  28.2 0.5 %shard_map.115 = (f32[2,192]{1,0:T(2,128)S(1)}, f32[2,192]{1,0:T(2,128)S(1)}) custom-call(f32[2,2048]{1,0:T(2,128)S(1)} %shard_map.114.mine_ref, f32[1,4096]{1,0:T(1,128)S(1)} %bitcast.16, bf16[192,4096]{1,0:T(8,128)(2,1)S(1)} %bitcast.10, bf16[192,4096]{1,0:T(8,128)(2,1)S(1)} %bitcast.12, bf16[192,4096]{1,0:T(8,128)(2,1)S(1)} %bitcast.14), custom_call_target="tpu_custom_call" | custom-call | flops 1024 | bytes 1024 | tf_op jit(solution)/shard_map/pallas_call | solution.py:345
  28.7 0.4 %collective-permute-done.1.came_ref = f32[2,2048]{1,0:T(2,128)S(1)} collective-permute-done((f32[2,2048]{1,0:T(2,128)S(1)}, f32[2,2048]{1,0:T(2,128)S(1)}, u32[]{:S(2)}, u32[]{:S(2)}) %collective-permute-start.1) | collective-permute-done | bytes 16416 | tf_op jit(solution)/shard_map/ppermute | solution.py:338
  29.2 0.0 copy-done.7
  29.2 0.8 %shard_map.116 = (bf16[2,4096]{1,0:T(2,128)(2,1)S(1)}, f32[2,128]{1,0:T(2,128)S(1)}) custom-call(f32[2,2048]{1,0:T(2,128)S(1)} %shard_map.114.mine_ref, f32[2,2048]{1,0:T(2,128)S(1)} %collective-permute-done.1.came_ref, f32[2,192]{1,0:T(2,128)S(1)} %get-tuple-element.19.gate_part, f32[2,192]{1,0:T(2,128)S(1)} %get-tuple-element.20.up_part, ...), custom_call_target="tpu_custom_call" | custom-call | flops 1024 | bytes 1024 | tf_op jit(solution)/shard_map/pallas_call | solution.py:348
  30.0 8.9 %all_to_all.17 = bf16[2,32,128]{2,0,1:T(2,128)(2,1)S(1)} all-to-all(bf16[2,32,128]{2,0,1:T(2,128)(2,1)S(1)} %bitcast.18), channel_id=1, replica_groups=mesh['group'=1,'ctx'=32] {'ctx'}, dimensions={1} | all-to-all | bytes 32768 | tf_op jit(solution)/shard_map/all_to_all | solution.py:368
  38.9 0.6 %add.3 = f32[2,128]{1,0:T(2,128)} add(f32[2,128]{1,0:T(2,128)S(1)} %get-tuple-element.21, f32[2,128]{1,0:T(2,128)S(1)} %convert_reduce_fusion) | non-fusion elementwise | flops 256 | bytes 3072 | tf_op jit(solution)/shard_map/add | solution.py:373
  (9 shorter events, 0.1 us)
Async XLA Ops:
  1.5 14.7 %copy-start = (bf16[256,4096]{1,0:T(8,128)(2,1)S(1)}, bf16[256,4096]{1,0:T(8,128)(2,1)}, u32[]{:S(2)}) copy-start(bf16[256,4096]{1,0:T(8,128)(2,1)} %weight_ref.3) | copy-start | bytes 6291460
  16.2 11.7 %copy-start.5 = (bf16[2,4096]{1,0:T(2,128)(2,1)S(1)}, bf16[2,4096]{1,0:T(2,128)(2,1)}, u32[]{:S(2)}) copy-start(bf16[2,4096]{1,0:T(2,128)(2,1)} %hidden_ref.1) | copy-start | bytes 49156
  16.2 12.0 %copy-start.2 = (bf16[1,4096,192]{1,2,0:T(8,128)(2,1)S(1)}, bf16[1,4096,192]{1,2,0:T(8,128)(2,1)}, u32[]{:S(2)}) copy-start(bf16[1,4096,192]{1,2,0:T(8,128)(2,1)} %param.18) | copy-start | bytes 4718596
  16.2 12.0 %copy-start.3 = (bf16[1,192,4096]{2,1,0:T(8,128)(2,1)S(1)}, bf16[1,192,4096]{2,1,0:T(8,128)(2,1)}, u32[]{:S(2)}) copy-start(bf16[1,192,4096]{2,1,0:T(8,128)(2,1)} %param.19) | copy-start | bytes 4718596
  16.7 11.5 %copy-start.1 = (bf16[1,4096,192]{1,2,0:T(8,128)(2,1)S(1)}, bf16[1,4096,192]{1,2,0:T(8,128)(2,1)}, u32[]{:S(2)}) copy-start(bf16[1,4096,192]{1,2,0:T(8,128)(2,1)} %param.17) | copy-start | bytes 4718596
  16.7 11.5 %copy-start.4 = (f32[4096]{0:T(1024)S(1)}, f32[4096]{0:T(1024)}, u32[]{:S(2)}) copy-start(f32[4096]{0:T(1024)} %param.16) | copy-start | bytes 49156
  16.7 1.2 %collective-permute-start = (f32[2,2048]{1,0:T(2,128)S(1)}, f32[2,2048]{1,0:T(2,128)S(1)}, u32[]{:S(2)}, u32[]{:S(2)}) collective-permute-start(f32[2,2048]{1,0:T(2,128)S(1)} %get-tuple-element.18), channel_id=1, source_target_pairs={{0,1},{1,0},{2,3},{3,2},{4,5},{5,4},{6,7},{7,6},{8,9},{9,8},{10,11... | collective-permute-start | bytes 49160 | tf_op jit(solution)/shard_map/ppermute | solution.py:331
  27.9 1.2 %collective-permute-start.1 = (f32[2,2048]{1,0:T(2,128)S(1)}, f32[2,2048]{1,0:T(2,128)S(1)}, u32[]{:S(2)}, u32[]{:S(2)}) collective-permute-start(f32[2,2048]{1,0:T(2,128)S(1)} %shard_map.114.mine_ref), channel_id=1, source_target_pairs={{0,1},{1,0},{2,3},{3,2},{4,5},{5,4},{6,7},{7,6},{8,9},{9,8},{10,11... | collective-permute-start | bytes 49160 | tf_op jit(solution)/shard_map/ppermute | solution.py:338
  28.2 1.0 %copy-start.6 = (s32[2,4]{1,0:T(2,128)S(1)}, s32[2,4]{1,0:T(2,128)}, u32[]{:S(2)}) copy-start(s32[2,4]{1,0:T(2,128)} %routes_ref.1) | copy-start | bytes 100
  28.2 0.9 %copy-start.7 = (f32[2,4]{1,0:T(2,128)S(1)}, f32[2,4]{1,0:T(2,128)}, u32[]{:S(2)}) copy-start(f32[2,4]{1,0:T(2,128)} %share_ref.1) | copy-start | bytes 100
